TPU v7x, 8 devices: a whole 2x2x1 slice. The times are simulated.
8 devices in a mesh: dp: 1 (over z), tp: 2 (over y), cp: 4 (over x, core).
Axes of the slice: x: 2, y: 2, z: 1, core: 2. Of those that a mesh axis runs over, the one named last changes fastest.
Arguments:
- x: bfloat16 [8192, 1536], P(('dp', 'cp', 'tp'))
- pos: int32 [8192], P(('dp', 'cp', 'tp'))
- g1: bfloat16 [1536], replicated
- g2: bfloat16 [1536], replicated
- wq: bfloat16 [1536, 1536], P(None, 'tp')
- wk: bfloat16 [1536, 256], P(None, 'tp')
- wv: bfloat16 [1536, 256], P(None, 'tp')
- wo: bfloat16 [1536, 1536], P('tp')
- w1: bfloat16 [1536, 8960], P(None, 'tp')
- w3: bfloat16 [1536, 8960], P(None, 'tp')
- w2: bfloat16 [8960, 1536], P('tp')
Outputs:
- output: bfloat16 [8192, 1536], P(('dp', 'cp', 'tp'))
All inputs are finite; a program needn't handle non-finite values.
Results may differ from a plain program's by a relative error of at most 0.00963285.
Values are sent between devices in bfloat16 or wider.
A program may use at most 1 GiB of HBM per device.

v0:
```python
import math
import jax
import jax.numpy as jnp
from jax import lax
from jax.sharding import PartitionSpec as P, NamedSharding

DH = 128
EPS = 1e-5
THETA = 500000.0


def rms_norm(v, g):
    vf = v.astype(jnp.float32)
    inv = lax.rsqrt(jnp.mean(vf * vf, axis=-1, keepdims=True) + EPS)
    return (vf * inv * g.astype(jnp.float32)).astype(jnp.bfloat16)


def rope(y, p):
    half = DH // 2
    freq = 1.0 / (THETA ** (jnp.arange(0, DH, 2, dtype=jnp.float32) / DH))
    ang = p.astype(jnp.float32)[..., None] * freq
    c = jnp.cos(ang)[..., None, :]
    s = jnp.sin(ang)[..., None, :]
    y1 = y[..., :half]
    y2 = y[..., half:]
    return jnp.concatenate([y1 * c - y2 * s, y2 * c + y1 * s], axis=-1)


def attend(q, k, v, qpos, kpos):
    nq, hl, dh = q.shape
    hk = k.shape[1]
    grp = hl // hk
    qb = nq
    while qb % 2 == 0 and qb * hl > 1024:
        qb = qb // 2
    qr = q.reshape(nq // qb, qb, hk, grp, dh)
    pr = qpos.reshape(nq // qb, qb)
    scale = 1.0 / math.sqrt(dh)

    def blk(qp):
        qq, pp = qp
        s = jnp.einsum('qkgd,skd->kgqs', qq, k, preferred_element_type=jnp.float32) * scale
        s = jnp.where(kpos[None, None, None, :] <= pp[None, None, :, None], s, -1e30)
        e = jnp.exp(s - jnp.max(s, axis=-1, keepdims=True))
        w = (e / jnp.sum(e, axis=-1, keepdims=True)).astype(jnp.bfloat16)
        o = jnp.einsum('kgqs,skd->qkgd', w, v, preferred_element_type=jnp.float32)
        return o.astype(jnp.bfloat16)

    return lax.map(blk, (qr, pr)).reshape(nq, hl * dh)


def solution(mesh):
    tok = P(('dp', 'cp', 'tp'), None)
    col = P(None, 'tp')
    row = P('tp', None)

    def local(x, pos, g1, g2, wq, wk, wv, wo, w1, w3, w2):
        a = lax.all_gather(rms_norm(x, g1), 'tp', axis=0, tiled=True)
        pg = lax.all_gather(pos, 'tp', axis=0, tiled=True)
        nr = a.shape[0]
        q = rope(jnp.dot(a, wq, preferred_element_type=jnp.float32).reshape(nr, -1, DH), pg).astype(jnp.bfloat16)
        k = rope(jnp.dot(a, wk, preferred_element_type=jnp.float32).reshape(nr, -1, DH), pg).astype(jnp.bfloat16)
        v = jnp.dot(a, wv, preferred_element_type=jnp.float32).astype(jnp.bfloat16).reshape(nr, -1, DH)
        ka = lax.all_gather(k, 'cp', axis=0, tiled=True)
        va = lax.all_gather(v, 'cp', axis=0, tiled=True)
        pa = lax.all_gather(pg, 'cp', axis=0, tiled=True)
        o = attend(q, ka, va, pg, pa)
        y = lax.psum_scatter(jnp.dot(o, wo, preferred_element_type=jnp.float32), 'tp', scatter_dimension=0, tiled=True)
        h1 = (x.astype(jnp.float32) + y).astype(jnp.bfloat16)
        b = lax.all_gather(rms_norm(h1, g2), 'tp', axis=0, tiled=True)
        hid = (jax.nn.silu(jnp.dot(b, w1, preferred_element_type=jnp.float32)) * jnp.dot(b, w3, preferred_element_type=jnp.float32)).astype(jnp.bfloat16)
        z = lax.psum_scatter(jnp.dot(hid, w2, preferred_element_type=jnp.float32), 'tp', scatter_dimension=0, tiled=True)
        return (h1.astype(jnp.float32) + z).astype(jnp.bfloat16)

    return jax.shard_map(local, mesh=mesh, in_specs=(tok, P(('dp', 'cp', 'tp')), P(None), P(None), col, col, col, row, col, col, row), out_specs=tok, check_vma=False)
```

profile of v0, /device:TPU:0, one launch (start us, length us, event | category | flops | bytes accessed | tf_op | source)
XLA Modules:
  0.0 1247.9 jit_solution(12265755186971864546)
XLA Ops:
  20.1 75.5 %all-gather.6.cloned.1.call-done = bf16[2048,1536]{1,0:T(8,128)(2,1)} async-done(((bf16[1024,1536]{1,0:T(8,128)(2,1)}), bf16[2048,1536]{1,0:T(8,128)(2,1)}) %all-gather.6.cloned.1.call-update) | async-done | bytes 6291472 | tf_op jit(solution)/shard_map/all_gather | solution.py:58
  145.0 588.1 %while.10 = (s32[]{:T(128)}, bf16[16,128,1,6,128]{4,1,3,2,0:T(8,128)(2,1)}, s32[8192]{0:T(1024)S(1)}, s32[16,128]{1,0:T(8,128)S(1)}, bf16[16,128,1,6,128]{4,1,3,...) while((s32[]{:T(128)}, ...), condition=%wide.region_4.5_spmd, body=%wide.region_1.4_spmd.sunk | while | flops 3297868288 | bytes 92717704 | solution.py:49
  158.1 12.0 fusion.82
  170.1 12.1 fusion.83
  182.9 11.9 fusion.81
  194.8 12.0 fusion.82
  206.8 12.1 fusion.83
  219.6 11.9 fusion.81
  231.5 12.0 fusion.82
  243.6 12.1 fusion.83
  256.3 11.9 fusion.81
  268.2 12.0 fusion.82
  280.3 12.1 fusion.83
  305.0 12.0 fusion.82
  317.0 12.1 fusion.83
  329.8 11.9 fusion.81
  341.7 12.0 fusion.82
  353.7 12.1 fusion.83
  378.4 12.0 fusion.82
  390.5 12.1 fusion.83
  403.2 11.9 fusion.81
  415.1 12.0 fusion.82
  427.2 12.1 fusion.83
  451.9 12.0 fusion.82
  463.9 12.1 fusion.83
  476.7 11.9 fusion.81
  488.6 12.0 fusion.82
  500.6 12.1 fusion.83
  525.3 12.0 fusion.82
  537.4 12.1 fusion.83
  562.0 12.0 fusion.82
  574.1 12.1 fusion.83
  586.9 11.9 fusion.81
  598.8 12.0 fusion.82
  610.8 12.1 fusion.83
  635.5 12.0 fusion.82
  647.5 12.1 fusion.83
  660.3 11.9 fusion.81
  672.2 12.0 fusion.82
  684.2 12.1 fusion.83
  708.9 12.0 fusion.82
  721.0 12.1 fusion.83
  749.0 141.2 %reduce-scatter.3.cloned.1.call-done = f32[1024,1536]{1,0:T(8,128)} async-done(((f32[2048,1536]{1,0:T(8,128)}), f32[1024,1536]{1,0:T(8,128)}) %reduce-scatter.3.cloned.1.call-update) | async-done | bytes 6291472 | tf_op jit(solution)/shard_map/reduce_scatter | solution.py:68
  899.2 78.3 %all-gather.10.cloned.1.call-done = bf16[2048,1536]{1,0:T(8,128)(2,1)} async-done(((bf16[1024,1536]{1,0:T(8,128)(2,1)}), bf16[2048,1536]{1,0:T(8,128)(2,1)}) %all-gather.10.cloned.1.call-update) | async-done | bytes 6291472 | tf_op jit(solution)/shard_map/all_gather | solution.py:70
  977.5 36.5 %fusion.51 = f32[2048,4480]{1,0:T(8,128)} fusion(bf16[2048,1536]{1,0:T(8,128)(2,1)} %all-gather.10.cloned.1.call-done, bf16[1536,4480]{1,0:T(8,128)(2,1)} %param.21), kind=kOutput, calls=%fused_computation.63 | convolution fusion | flops 28185722880 | bytes 56754176 | tf_op jit(solution)/shard_map/dot_general | solution.py:71
  1014.0 40.6 %multiply_convert_fusion.clone.4 = bf16[2048,4480]{1,0:T(8,128)(2,1)} fusion(f32[2048,4480]{1,0:T(8,128)} %fusion.51, bf16[2048,1536]{1,0:T(8,128)(2,1)} %all-gather.10.cloned.1.call-done, bf16[1536,4480]{1,0:T(8,128)(2,1)} %param.22), kind=kOutput, calls=%fused_computation.21.clone.clone.clone.1 | convolution fusion | flops 28240773120 | bytes 75104256 | tf_op jit(solution)/shard_map/dot_general | solution.py:71
  1054.6 38.0 %fusion.28 = f32[2048,1536]{1,0:T(8,128)} fusion(bf16[4480,1536]{1,0:T(8,128)(2,1)} %param.23, bf16[2048,4480]{1,0:T(8,128)(2,1)} %multiply_convert_fusion.clone.4), kind=kOutput, calls=%fused_computation.22 | convolution fusion | flops 28185722880 | bytes 44695552 | tf_op jit(solution)/shard_map/dot_general | solution.py:72
  1092.6 141.8 %reduce-scatter.5.cloned.1.call-done = f32[1024,1536]{1,0:T(8,128)} async-done(((f32[2048,1536]{1,0:T(8,128)}), f32[1024,1536]{1,0:T(8,128)}) %reduce-scatter.5.cloned.1.call-update) | async-done | bytes 6291472 | tf_op jit(solution)/shard_map/reduce_scatter | solution.py:72
  (128 shorter events, 199.7 us)
Async XLA Ops:
  6.5 731.5 %copy-start = (bf16[768,1536]{1,0:T(8,128)(2,1)S(1)}, bf16[768,1536]{1,0:T(8,128)(2,1)}, u32[]{:S(2)}) copy-start(bf16[768,1536]{1,0:T(8,128)(2,1)} %param.20) | copy-start | bytes 7077892
  6.5 7.9 copy-start.4
  6.5 89.0 %copy-start.3 = (bf16[1536,128]{1,0:T(8,128)(2,1)S(1)}, bf16[1536,128]{1,0:T(8,128)(2,1)}, u32[]{:S(2)}) copy-start(bf16[1536,128]{1,0:T(8,128)(2,1)} %param.18) | copy-start | bytes 1179652
  6.5 89.0 %all-gather.6.cloned.1.call-start = ((), (), s32[]{:S(2)}) async-start(), calls=%async_computation.2 | async-start | bytes 9437184 | tf_op jit(solution)/shard_map/all_gather | solution.py:58
  14.3 122.6 %all-gather.8.cloned.1.call-start = ((), (), s32[]{:S(2)}) async-start(), calls=%async_computation.3 | async-start | bytes 2621440 | tf_op jit(solution)/shard_map/all_gather | solution.py:64
  20.1 83.7 %copy-start.7 = (bf16[1536,128]{1,0:T(8,128)(2,1)S(1)}, bf16[1536,128]{1,0:T(8,128)(2,1)}, u32[]{:S(2)}) copy-start(bf16[1536,128]{1,0:T(8,128)(2,1)} %param.19) | copy-start | bytes 1179652
  103.8 41.2 %all-gather.12.cloned.1.call-start = ((), (), s32[]{:S(2)}) async-start(), calls=%async_computation.7 | async-start | bytes 2621440 | tf_op jit(solution)/shard_map/all_gather | solution.py:65
  109.3 780.9 %reduce-scatter.3.cloned.1.call-start = ((), (), s32[]{:S(2)}) async-start(), calls=%async_computation.4 | async-start | bytes 18874368 | tf_op jit(solution)/shard_map/reduce_scatter | solution.py:68
  158.1 12.0 copy-start.6
  194.8 12.0 copy-start.6
  231.5 12.0 copy-start.6
  268.2 12.0 copy-start.6
  305.0 12.0 copy-start.6
  341.7 12.0 copy-start.6
  378.4 12.0 copy-start.6
  415.1 12.0 copy-start.6
  451.9 12.0 copy-start.6
  488.6 12.0 copy-start.6
  525.3 12.0 copy-start.6
  562.0 12.0 copy-start.6
  598.8 12.0 copy-start.6
  635.5 12.0 copy-start.6
  672.2 12.0 copy-start.6
  708.9 12.0 copy-start.6
  748.3 0.7 copy-start.5
  748.4 229.1 %all-gather.10.cloned.1.call-start = ((), (), s32[]{:S(2)}) async-start(), calls=%async_computation.5 | async-start | bytes 9437184 | tf_op jit(solution)/shard_map/all_gather | solution.py:70
  894.9 1.8 copy-start.2
  899.1 335.3 %reduce-scatter.5.cloned.1.call-start = ((), (), s32[]{:S(2)}) async-start(), calls=%async_computation.6 | async-start | bytes 18874368 | tf_op jit(solution)/shard_map/reduce_scatter | solution.py:72
  1092.6 148.2 %copy-start.1 = (bf16[768,1536]{1,0:T(8,128)(2,1)S(1)}, bf16[768,1536]{1,0:T(8,128)(2,1)}, u32[]{:S(2)}) copy-start(bf16[768,1536]{1,0:T(8,128)(2,1)} %param.20) | copy-start | bytes 7077892
Sparse Core Ops, SparseCore 0:
  14.5 81.0 all-gather.5
  103.9 19.9 all-gather.7
  125.4 19.5 all-gather.11
  748.5 141.6 reduce-scatter.2
  899.2 78.2 all-gather.9
  1092.7 141.6 reduce-scatter.4
where the time goes:
time: 1250 us
  matrix products  528 us (42%)
  waiting for transfers between devices  441 us (35%)
  other arithmetic  232 us (19%)
  local copies, waits for them, and re-layouts  17.1 us (1%)
  blocking collectives  14.5 us (1%)
  between operations  13.8 us (1%)
    dot_general x16, matrix products, blk(): o = jnp.einsum('kgqs,skd->qkgd', w, v, preferred_element_type=jnp.float32)  194 us
    reduce_sum x16, other arithmetic, blk(): w = (e / jnp.sum(e, axis=-1, keepdims=True)).astype(jnp.bfloat16)  193 us
    dot_general x16, matrix products, blk(): jnp.einsum('qkgd,skd->kgqs', qq, k, preferred_element_type=jnp.float32)  190 us
    reduce_scatter x1, waiting for transfers between devices, local(): lax.psum_scatter(jnp.dot(hid, w2, preferred_element_type=jnp.float32), 't...  142 us
    reduce_scatter x1, waiting for transfers between devices, local(): lax.psum_scatter(jnp.dot(o, wo, preferred_element_type=jnp.float32), 'tp'...  141 us
    all_gather x1, waiting for transfers between devices, local(): b = lax.all_gather(rms_norm(h1, g2), 'tp', axis=0, tiled=True)  78.3 us
    all_gather x1, waiting for transfers between devices, local(): a = lax.all_gather(rms_norm(x, g1), 'tp', axis=0, tiled=True)  75.5 us
    dot_general x1, matrix products, local(): jnp.dot(b, w3, preferred_element_type=jnp.float32)  40.6 us
  transfers between devices with their start and end apart: 6, of which 5 were waited for; matrix products, arithmetic and copies ran while one was open for 2% of the time, Pallas kernels for 0%

commit v1 on v0

v1 whole, which is shorter than its diff:
```python
import functools
import math
import jax
import jax.numpy as jnp
from jax import lax
from jax.experimental import pallas as pl
from jax.experimental.pallas import tpu as pltpu
from jax.sharding import PartitionSpec as P

DH = 128
EPS = 1e-5
THETA = 500000.0
NEG = -1e30
LC = math.log2(math.e) / math.sqrt(DH)
PC = 512
GRP = 6


def rms_norm(v, g):
    vf = v.astype(jnp.float32)
    inv = lax.rsqrt(jnp.mean(vf * vf, axis=-1, keepdims=True) + EPS)
    return (vf * inv * g.astype(jnp.float32)).astype(jnp.bfloat16)


def rope(y, c, s):
    half = DH // 2
    y1 = y[..., :half]
    y2 = y[..., half:]
    return jnp.concatenate([y1 * c - y2 * s, y2 * c + y1 * s], axis=-1)


def attn_kernel(nsrc, masked, first, last, tab, *refs):
    refs = list(refs)
    q_ref = refs.pop(0)
    k_refs = [refs.pop(0) for _ in range(nsrc)]
    v_refs = [refs.pop(0) for _ in range(nsrc)]
    if not first:
        ai_ref = refs.pop(0)
        mi_ref = refs.pop(0)
    if last:
        o_ref = refs.pop(0)
    else:
        ao_ref = refs.pop(0)
        mo_ref = refs.pop(0)
    m_s, al_s, acc_s, ks, vs, s0, s1, p0, p1 = refs
    S = [s0, s1]
    PP = [p0, p1]
    units = 2 * nsrc + (1 if masked else 0)
    for i in range(nsrc):
        ks[i * 1024:(i + 1) * 1024, :] = k_refs[i][...]
        vs[i * 1024:(i + 1) * 1024, :] = v_refs[i][...]
    if first:
        m_s[...] = jnp.full_like(m_s, NEG)
        acc_s[...] = jnp.zeros_like(acc_s)
    else:
        for qp in range(2):
            for h in range(GRP):
                m_s[qp, h] = jnp.broadcast_to(mi_ref[qp, :, h:h + 1], (PC, 128))
                acc_s[qp, h, :, :128] = ai_ref[qp, h]
                acc_s[qp, h, :, 128:] = jnp.broadcast_to(mi_ref[qp, :, 64 + h:65 + h], (PC, 128))
    al_s[...] = jnp.ones_like(al_s)
    p1[...] = jnp.zeros_like(p1)
    ones = jnp.ones((PC, 128), jnp.bfloat16)

    def qk(u, h):
        qo = pl.multiple_of(tab[u, 0] * PC, PC)
        ko = pl.multiple_of(tab[u, 1] * PC, PC)
        S[h % 2][...] = lax.dot_general(q_ref[pl.ds(qo, PC), h * 128:(h + 1) * 128], ks[pl.ds(ko, PC), :],
                                        (((1,), (1,)), ((), ())), preferred_element_type=jnp.float32)

    def sm(u, h):
        qp = tab[u, 0]
        s = S[h % 2][...]
        if masked:
            r = lax.broadcasted_iota(jnp.int32, s.shape, 0)
            c = lax.broadcasted_iota(jnp.int32, s.shape, 1)
            s = jnp.where(c - r <= tab[u, 2], s, NEG)
        mx = jnp.max(s, axis=1, keepdims=True)
        mp = m_s[qp, h]
        mn = jnp.maximum(mp, mx)
        al_s[h % 2] = jnp.exp2((mp - mn) * LC)
        pr = jnp.exp2(s * LC - jnp.tile(mn * LC, (1, PC // 128)))
        PP[h % 2][...] = pr.astype(jnp.bfloat16)
        m_s[qp, h] = mn

    def pv(u, h):
        qp = tab[u, 0]
        ko = pl.multiple_of(tab[u, 1] * PC, PC)
        vb = jnp.concatenate([vs[pl.ds(ko, PC), :], ones], axis=1)
        x = jnp.dot(PP[h % 2][...], vb, preferred_element_type=jnp.float32)
        acc_s[qp, h] = acc_s[qp, h] * jnp.tile(al_s[h % 2], (1, 2)) + x

    qk(0, 0)

    def body(u, _):
        for h in range(GRP):
            qk(u if h < GRP - 1 else jnp.minimum(u + 1, units - 1), (h + 1) % GRP)
            pv(jnp.maximum(u - 1, 0) if h == 0 else u, (h - 1) % GRP)
            sm(u, h)
        return 0

    lax.fori_loop(0, units, body, 0)
    pv(units - 1, GRP - 1)
    if last:
        for qp in range(2):
            for h in range(GRP):
                a = acc_s[qp, h]
                o_ref[qp * PC:(qp + 1) * PC, h * 128:(h + 1) * 128] = (a[:, :128] / a[:, 128:]).astype(jnp.bfloat16)
    else:
        lane = lax.broadcasted_iota(jnp.int32, (PC, 128), 1)
        for qp in range(2):
            ml = jnp.zeros((PC, 128), jnp.float32)
            for h in range(GRP):
                ao_ref[qp, h] = acc_s[qp, h, :, :128]
                ml = jnp.where(lane == h, m_s[qp, h], ml)
                ml = jnp.where(lane == 64 + h, acc_s[qp, h, :, 128:], ml)
            mo_ref[qp] = ml


def attn_call(tab, q, ks, vs, state, masked, last, name):
    nsrc = len(ks)
    first = state is None
    qs = pl.BlockSpec((1024, 768), lambda g, t: (0, g))
    kv = pl.BlockSpec((1024, 128), lambda g, t: (0, g))
    sa = pl.BlockSpec((None, 2, GRP, PC, 128), lambda g, t: (g, 0, 0, 0, 0))
    sml = pl.BlockSpec((None, 2, PC, 128), lambda g, t: (g, 0, 0, 0))
    ins = [qs] + [kv] * (2 * nsrc) + ([] if first else [sa, sml])
    if last:
        outs = qs
        osh = jax.ShapeDtypeStruct((1024, 1536), jnp.bfloat16)
    else:
        outs = [sa, sml]
        osh = [jax.ShapeDtypeStruct((2, 2, GRP, PC, 128), jnp.float32), jax.ShapeDtypeStruct((2, 2, PC, 128), jnp.float32)]
    units = 2 * nsrc + (1 if masked else 0)
    return pl.pallas_call(
        functools.partial(attn_kernel, nsrc, masked, first, last),
        grid_spec=pltpu.PrefetchScalarGridSpec(
            num_scalar_prefetch=1, grid=(2,), in_specs=ins, out_specs=outs,
            scratch_shapes=[
                pltpu.VMEM((2, GRP, PC, 128), jnp.float32), pltpu.VMEM((2, PC, 128), jnp.float32),
                pltpu.VMEM((2, GRP, PC, 256), jnp.float32),
                pltpu.VMEM((nsrc * 1024, 128), jnp.bfloat16), pltpu.VMEM((nsrc * 1024, 128), jnp.bfloat16),
                pltpu.VMEM((PC, PC), jnp.float32), pltpu.VMEM((PC, PC), jnp.float32),
                pltpu.VMEM((PC, PC), jnp.bfloat16), pltpu.VMEM((PC, PC), jnp.bfloat16)]),
        out_shape=osh,
        compiler_params=pltpu.CompilerParams(vmem_limit_bytes=60 * 2**20),
        cost_estimate=pl.CostEstimate(flops=units * 12 * 2 * PC * PC * 512, bytes_accessed=20 * 2**20, transcendentals=units * 12 * PC * PC),
        name=name)(tab, q, *ks, *vs, *([] if first else state))


def solution(mesh):
    tok = P(('dp', 'cp', 'tp'), None)
    col = P(None, 'tp')
    row = P('tp', None)
    ncp = mesh.shape['cp']
    ntp = mesh.shape['tp']

    def perm(v, dc, dj):
        pairs = []
        for c in range(ncp):
            for j in range(ntp):
                pairs.append((j * ncp + c, (j ^ dj) * ncp + (c ^ dc)))
        return lax.ppermute(v, ('tp', 'cp'), pairs)

    def local(x, pos, g1, g2, wq, wk, wv, wo, w1, w3, w2):
        c = lax.axis_index('cp')
        j = lax.axis_index('tp')
        k = c * ntp + j
        core = c % 2

        def other_half(w):
            n = w.shape[0] // 2
            mine = lax.dynamic_slice_in_dim(w, core * n, n, 0)
            got = perm(mine, 0, 1)
            sib = perm(got, 1, 0)
            return jnp.where(core == 0, jnp.concatenate([got, sib], 0), jnp.concatenate([sib, got], 0))

        wkv = jnp.concatenate([wk, wv], 1)
        wkv_o = other_half(wkv)
        wq_o = other_half(wq)
        wo_o = other_half(wo)

        a = rms_norm(x, g1)
        freq = 1.0 / (THETA ** (jnp.arange(0, DH, 2, dtype=jnp.float32) / DH))
        ang = pos.astype(jnp.float32)[:, None] * freq
        cs = jnp.cos(ang)[:, None, :]
        sn = jnp.sin(ang)[:, None, :]

        def proj(w):
            return jnp.dot(a, w, preferred_element_type=jnp.float32)

        def swap(m, o, ax=1):
            return jnp.where(j == 0, jnp.concatenate([m, o], ax), jnp.concatenate([o, m], ax))

        kvm = proj(wkv)
        kvo = proj(wkv_o)

        def kpart(y):
            return rope(y[:, :DH].reshape(1024, 1, DH), cs, sn).astype(jnp.bfloat16).reshape(1024, DH)

        kk = swap(kpart(kvm), kpart(kvo))
        vv = swap(kvm[:, DH:].astype(jnp.bfloat16), kvo[:, DH:].astype(jnp.bfloat16))
        kva = jnp.concatenate([kk, vv], 1)
        kvs = perm(kva, 1, 0)
        kvx = perm(kva, 2, 0)
        kvy = perm(kva, 0, 1)
        kvxs = perm(kvx, 1, 0)
        kvys = perm(kvy, 1, 0)
        z1 = perm(kvx[:512], 0, 1)
        z2 = perm(kvy[512:], 2, 0)
        kvz = jnp.concatenate([z1, z2], 0)
        kvzs = perm(kvz, 1, 0)

        def qpart(w):
            return rope(proj(w).reshape(1024, GRP, DH), cs, sn).astype(jnp.bfloat16).reshape(1024, GRP * DH)

        q = swap(qpart(wq), qpart(wq_o))

        def units(devs, base):
            rows = []
            for i, d in enumerate(devs):
                gt = d > k
                rows.append(jnp.stack([jnp.where(gt, 1, 0), jnp.int32(2 * (i + base)), jnp.int32(PC)]))
                rows.append(jnp.stack([jnp.int32(1), jnp.where(gt, 2 * (i + base) + 1, 2 * (i + base)), jnp.int32(PC)]))
            return rows

        def dev(dc, dj):
            return (c ^ dc) * ntp + (j ^ dj)

        t1 = jnp.stack([jnp.array([0, 0, 0], jnp.int32), jnp.array([1, 1, 0], jnp.int32), jnp.array([1, 0, PC], jnp.int32)]
                       + units([dev(1, 0)], 1)).astype(jnp.int32)
        t2 = jnp.stack(units([dev(2, 0), dev(3, 0), dev(0, 1), dev(1, 1)], 0)).astype(jnp.int32)
        t3 = jnp.stack(units([dev(2, 1), dev(3, 1)], 0)).astype(jnp.int32)
        sp = lambda t: (t[:, :256], t[:, 256:])
        st = attn_call(t1, q, *zip(*map(sp, [kva, kvs])), None, True, False, "attn1")
        st = attn_call(t2, q, *zip(*map(sp, [kvx, kvxs, kvy, kvys])), st, False, False, "attn2")
        o = attn_call(t3, q, *zip(*map(sp, [kvz, kvzs])), st, False, True, "attn3")

        wof = swap(wo, wo_o, 0)
        h1 = (x.astype(jnp.float32) + jnp.dot(o, wof, preferred_element_type=jnp.float32)).astype(jnp.bfloat16)
        hp = [perm(h1[:512], 0, 1), perm(h1[512:], 0, 1)]

        def mlp(h):
            b = rms_norm(h, g2)
            hid = (jax.nn.silu(jnp.dot(b, w1, preferred_element_type=jnp.float32)) * jnp.dot(b, w3, preferred_element_type=jnp.float32)).astype(jnp.bfloat16)
            return jnp.dot(hid, w2, preferred_element_type=jnp.float32)

        zp = [perm(mlp(h).astype(jnp.bfloat16), 0, 1) for h in hp]
        z = mlp(h1)
        zr = jnp.concatenate(zp, 0).astype(jnp.float32)
        return (h1.astype(jnp.float32) + (z + zr)).astype(jnp.bfloat16)

    return jax.shard_map(local, mesh=mesh, in_specs=(tok, P(('dp', 'cp', 'tp')), P(None), P(None), col, col, col, row, col, col, row), out_specs=tok, check_vma=False)
```

time: 1250 us -> 427 us (0.34)
  waiting for transfers between devices: 441 us -> 65.1 us
  matrix products: 528 us -> 169 us
  other arithmetic: 232 us -> 23.9 us
  Pallas kernels: 0 us -> 109 us
  local copies, waits for them, and re-layouts: 17.1 us -> 38.7 us
  starting transfers between devices: 0.38 us -> 16 us
  blocking collectives: 14.5 us -> 0 us
  between operations: 13.8 us -> 0.76 us
    dot_general x39 -> x12, matrix products: 528 us -> 169 us  [the longest x3 75.4 us: mlp(): return jnp.dot(hid, w2, preferred_element_type=jnp.float32)]
    reduce_scatter x2 -> x0, waiting for transfers between devices: 283 us -> none  [the longest x1 142 us: local(): lax.psum_scatter(jnp.dot(hid, w2, preferred_element_type=jnp.float32), 't...]
    reduce_sum x16 -> x0, other arithmetic: 193 us -> none  [blk(): w = (e / jnp.sum(e, axis=-1, keepdims=True)).astype(jnp.bfloat16)]
    all_gather x4 -> x0, waiting for transfers between devices: 158 us -> none  [the longest x1 78.3 us: local(): b = lax.all_gather(rms_norm(h1, g2), 'tp', axis=0, tiled=True)]
    pallas_call x0 -> x3, Pallas kernels: none -> 109 us  [attn_call(): pl.pallas_call(functools.partial(attn_kernel, nsrc, masked, first, last),...]
    ppermute x0 -> x18, waiting for transfers between devices: none -> 65.1 us  [perm(): return lax.ppermute(v, ('tp', 'cp'), pairs)]
    slice x0 -> x12, local copies, waits for them, and re-layouts: none -> 21.7 us  [the longest x7 14.6 us: local(): sp = lambda t: (t[:, :256], t[:, 256:])]
    ppermute x0 -> x18, starting transfers between devices: none -> 16 us  [perm(): return lax.ppermute(v, ('tp', 'cp'), pairs)]
  transfers between devices with their start and end apart: 6 -> 18, of which waited for: 5 -> 5; matrix products, arithmetic and copies ran while one was open for 2% -> 45% of each run, Pallas kernels for 0% -> 19%
where the time goes in v1:
time: 427 us; the launch traced here: 423 us
  matrix products  169 us (40%)
  Pallas kernels  109 us (26%)
  waiting for transfers between devices  65.1 us (15%)
  local copies, waits for them, and re-layouts  38.7 us (9%)
  other arithmetic  23.9 us (6%)
  starting transfers between devices  16 us (4%)
    pallas_call x3, Pallas kernels, attn_call(): pl.pallas_call(functools.partial(attn_kernel, nsrc, masked, first, last),...  109 us
    dot_general x3, matrix products, mlp(): return jnp.dot(hid, w2, preferred_element_type=jnp.float32)  75.4 us
    ppermute x18, waiting for transfers between devices, perm(): return lax.ppermute(v, ('tp', 'cp'), pairs)  65.1 us
    dot_general x3, matrix products, mlp(): jnp.dot(b, w1, preferred_element_type=jnp.float32)  43.8 us
    dot_general x1, matrix products, mlp(): jnp.dot(b, w3, preferred_element_type=jnp.float32)  23.6 us
    dot_general x4, matrix products, proj(): return jnp.dot(a, w, preferred_element_type=jnp.float32)  17 us
    ppermute x18, starting transfers between devices, perm(): return lax.ppermute(v, ('tp', 'cp'), pairs)  16 us
    slice x7, local copies, waits for them, and re-layouts, local(): sp = lambda t: (t[:, :256], t[:, 256:])  14.6 us
  transfers between devices with their start and end apart: 18, of which 5 were waited for; matrix products, arithmetic and copies ran while one was open for 45% of the time, Pallas kernels for 19%

profile of v1, /device:TPU:0, one launch (start us, length us, event | category | flops | bytes accessed | tf_op | source)
XLA Modules:
  0.0 423.0 jit_solution(3861863224022367358)
XLA Ops:
  3.2 3.4 collective-permute-start.2
  7.7 1.4 constant_dynamic-slice_fusion
  9.0 2.0 collective-permute-start.12
  11.1 2.6 fusion.2
  16.8 4.1 fusion.98
  21.5 1.8 slice.189
  25.0 3.4 fusion.42
  28.5 2.8 fusion.76
  34.2 1.9 collective-permute-start.4
  36.1 4.6 %fusion.101 = f32[1024,768]{0,1:T(8,128)} fusion(bf16[1536,768]{1,0:T(8,128)(2,1)S(1)} %copy-done, bf16[1024,1536]{1,0:T(8,128)(2,1)S(1)} %copy-done.3, f32[1536]{0:T(1024)S(1)} %convert_element_type.82, f32[1024]{0:T(1024)S(1)} %copy-done.18), kind=kOutput, calls=%fused_computation.160 | convolution fusion | flops 2422210560 | bytes 8660992 | tf_op jit(solution)/shard_map/dot_general | solution.py:190
  43.2 1.3 stack.175.tab
  44.5 1.3 pad_add_fusion.tab
  45.7 1.7 multiply_cosine_fusion.1
  47.4 19.7 %collective-permute-done.12 = bf16[384,1536]{1,0:T(8,128)(2,1)} collective-permute-done((bf16[384,1536]{1,0:T(8,128)(2,1)S(1)}, bf16[384,1536]{1,0:T(8,128)(2,1)}, u32[]{:S(2)}, u32[]{:S(2)}) %collective-permute-start.12) | collective-permute-done | bytes 1179680 | tf_op jit(solution)/shard_map/ppermute | solution.py:163
  67.1 1.9 slice.134
  69.0 2.0 collective-permute-start.5
  71.0 18.6 %collective-permute-done.6 = bf16[1024,512]{1,0:T(8,128)(2,1)} collective-permute-done((bf16[1024,512]{1,0:T(8,128)(2,1)}, bf16[1024,512]{1,0:T(8,128)(2,1)}, u32[]{:S(2)}, u32[]{:S(2)}) %collective-permute-start.6) | collective-permute-done | bytes 1048608 | tf_op jit(solution)/shard_map/ppermute | solution.py:163
  89.6 1.9 slice.135
  91.4 2.0 collective-permute-start.7
  93.4 2.2 fusion.106
  95.6 2.3 fusion.108
  99.5 5.0 %fusion.27 = f32[1024,768]{0,1:T(8,128)S(1)} fusion(bf16[768,768]{1,0:T(8,128)(2,1)S(1)} %collective-permute-done.1, bf16[768,768]{1,0:T(8,128)(2,1)} %collective-permute-done, pred[]{:T(512)S(6)} %eq.7, bf16[1024,1536]{1,0:T(8,128)(2,1)S(1)} %copy-done.4, f32[1536]{0:T(1024)S(1)} %copy-done.14, f32[1024]{0:T(1024)S(1)} %copy-done.18), kind=kOutput, calls=%fused_computation.43 | convolution fusion | flops 2432827392 | bytes 8660993 | tf_op jit(solution)/shard_map/dot_general | solution.py:190
  105.6 1.5 pad_maximum_fusion
  107.8 1.7 copy.24
  109.6 1.9 constant_dynamic-update-slice_fusion.3
  111.5 1.9 constant_dynamic-update-slice_fusion.2
  113.3 2.0 maximum_select_fusion.4.refs_0_
  115.4 34.1 %attn1.1 = (f32[2,2,6,512,128]{4,3,2,1,0:T(8,128)}, f32[2,2,512,128]{3,2,1,0:T(8,128)}) custom-call(s32[5,3]{1,0:T(8,128)} %stack.185.tab, bf16[1024,1536]{1,0:T(8,128)(2,1)} %maximum_select_fusion.4.refs_0_, bf16[1024,256]{1,0:T(8,128)(2,1)} %copy-done.8, bf16[1024,256]{1,0:T(8,128)(2,1)} %get-tuple-element.20.refs_2_, bf16[1024,256]{1,0:T(8,128)(2,1)} %copy-done.9, ...), custom_call_target="tpu_custom_call" | custom-call | flops 16106127360 | bytes 20971520 | tf_op jit(solution)/shard_map/attn1/pallas_call | solution.py:135
  149.5 2.3 fusion.110
  151.8 3.6 maximum_select_fusion.7
  155.4 2.3 fusion.105
  157.7 2.3 fusion.107
  159.9 46.9 %attn2.1 = (f32[2,2,6,512,128]{4,3,2,1,0:T(8,128)}, f32[2,2,512,128]{3,2,1,0:T(8,128)}) custom-call(s32[8,3]{1,0:T(8,128)} %stack.175.tab, bf16[1024,1536]{1,0:T(8,128)(2,1)} %maximum_select_fusion.4.refs_0_, bf16[1024,256]{1,0:T(8,128)(2,1)} %get-tuple-element.28.refs_1_, bf16[1024,256]{1,0:T(8,128)(2,1)} %get-tuple-element.26.refs_2_, ...), custom_call_target="tpu_custom_call" | custom-call | flops 25769803776 | bytes 20971520 | tf_op jit(solution)/shard_map/attn2/pallas_call | solution.py:135
  206.9 2.2 fusion.109
  209.1 28.3 %attn3.1 = bf16[1024,1536]{1,0:T(8,128)(2,1)} custom-call(s32[4,3]{1,0:T(4,128)} %pad_add_fusion.tab, bf16[1024,1536]{1,0:T(8,128)(2,1)} %maximum_select_fusion.4.refs_0_, bf16[1024,256]{1,0:T(8,128)(2,1)} %get-tuple-element.32.refs_1_, bf16[1024,256]{1,0:T(8,128)(2,1)} %get-tuple-element.30.refs_2_, bf16[1024,256]{1,0:T(8,128)(2,1)} %get-tuple-element.31.refs_3_, ...), custom_call_target="tpu_custom_call" | custom-call | flops 12884901888 | bytes 20971520 | tf_op jit(solution)/shard_map/attn3/pallas_call | solution.py:135
  237.4 9.2 %fusion.6 = (f32[1024]{0:T(1024)S(1)}, bf16[1024,1536]{1,0:T(8,128)(2,1)S(1)}) fusion(bf16[1024,1536]{1,0:T(8,128)(2,1)} %attn3.1, bf16[768,1536]{1,0:T(8,128)(2,1)} %maximum_select_fusion.7, bf16[768,1536]{1,0:T(8,128)(2,1)} %param.21, pred[]{:T(512)S(6)} %eq.6, bf16[1024,1536]{1,0:T(8,128)(2,1)S(1)} %copy-done.5), kind=kOutput, calls=%fused_computation.15 | convolution fusion | flops 4862508032 | bytes 14159873 | tf_op jit(solution)/shard_map/dot_general | solution.py:240
  246.6 1.5 fusion.103
  248.2 1.5 collective-permute-start.14
  250.3 20.5 %fusion.35 = f32[1024,4480]{1,0:T(8,128)} fusion(bf16[1536,4480]{1,0:T(8,128)(2,1)} %param.22, bf16[1024,1536]{1,0:T(8,128)(2,1)S(1)} %get-tuple-element.44, f32[1536]{0:T(1024)S(1)} %convert_element_type.89, f32[1024]{0:T(1024)S(1)} %add_rsqrt_fusion), kind=kOutput, calls=%fused_computation.58 | convolution fusion | flops 14099152896 | bytes 35268608 | tf_op jit(solution)/shard_map/dot_general | solution.py:245
  270.7 14.7 %collective-permute-done.14 = bf16[512,1536]{1,0:T(8,128)(2,1)S(1)} collective-permute-done((bf16[512,1536]{1,0:T(8,128)(2,1)S(1)}, bf16[512,1536]{1,0:T(8,128)(2,1)S(1)}, u32[]{:S(2)}, u32[]{:S(2)}) %collective-permute-start.14) | collective-permute-done | bytes 1572896 | tf_op jit(solution)/shard_map/ppermute | solution.py:163
  285.9 10.3 %fusion.71 = f32[512,4480]{1,0:T(8,128)} fusion(bf16[1536,4480]{1,0:T(8,128)(2,1)S(1)} %bitcast.78, bf16[512,1536]{1,0:T(8,128)(2,1)S(1)} %collective-permute-done.14, f32[1536]{0:T(1024)S(1)} %convert_element_type.89, f32[512]{0:T(512)S(1)} %add_rsqrt_fusion.3), kind=kOutput, calls=%fused_computation.93 | convolution fusion | flops 7049576448 | bytes 24518656 | tf_op jit(solution)/shard_map/dot_general | solution.py:245
  296.2 26.3 %fusion.26 = bf16[512,1536]{1,0:T(8,128)(2,1)} fusion(bf16[4480,1536]{1,0:T(8,128)(2,1)} %param.24, f32[512,4480]{1,0:T(8,128)} %fusion.71, bf16[1536,4480]{1,0:T(8,128)(2,1)} %param.23, bf16[512,1536]{1,0:T(8,128)(2,1)S(1)} %collective-permute-done.14, f32[1536]{0:T(1024)S(1)} %convert_element_type.89, f32[512]{0:T(512)S(1)} %add_rsqrt_fusion.3), kind=kOutput, calls=%fused_computation.41 | convolution fusion | flops 14110556160 | bytes 39854080 | tf_op jit(solution)/shard_map/dot_general | solution.py:246
  322.5 1.5 collective-permute-start.15
  325.2 13.1 %fusion.67 = f32[512,4480]{1,0:T(8,128)} fusion(bf16[1536,4480]{1,0:T(8,128)(2,1)} %param.22, bf16[512,1536]{1,0:T(8,128)(2,1)S(1)} %collective-permute-done.16, f32[512]{0:T(512)S(1)} %add_rsqrt_fusion.2, f32[1536]{0:T(1024)S(1)} %convert_element_type.89), kind=kOutput, calls=%fused_computation.92 | convolution fusion | flops 7049576448 | bytes 24518656 | tf_op jit(solution)/shard_map/dot_general | solution.py:245
  338.3 27.0 %fusion.25 = bf16[512,1536]{1,0:T(8,128)(2,1)} fusion(bf16[4480,1536]{1,0:T(8,128)(2,1)} %param.24, f32[512,4480]{1,0:T(8,128)} %fusion.67, bf16[1536,4480]{1,0:T(8,128)(2,1)} %param.23, bf16[512,1536]{1,0:T(8,128)(2,1)} %copy-done.10, f32[512]{0:T(512)S(1)} %add_rsqrt_fusion.2, f32[1536]{0:T(1024)S(1)} %convert_element_type.89), kind=kOutput, calls=%fused_computation.40 | convolution fusion | flops 14110556160 | bytes 39854080 | tf_op jit(solution)/shard_map/dot_general | solution.py:246
  365.8 23.6 %multiply_convert_fusion.clone.6 = bf16[1024,4480]{1,0:T(8,128)(2,1)} fusion(f32[1024,4480]{1,0:T(8,128)} %fusion.35, bf16[1536,4480]{1,0:T(8,128)(2,1)} %param.23, bf16[1024,1536]{1,0:T(8,128)(2,1)S(1)} %copy-done.7, f32[1536]{0:T(1024)S(1)} %convert_element_type.89, f32[1024]{0:T(1024)S(1)} %add_rsqrt_fusion), kind=kOutput, calls=%fused_computation.clone.clone.clone.clone.clone.1 | convolution fusion | flops 14126678016 | bytes 44443648 | tf_op jit(solution)/shard_map/dot_general | solution.py:245
  389.4 11.1 %collective-permute-done.17 = bf16[512,1536]{1,0:T(8,128)(2,1)} collective-permute-done((bf16[512,1536]{1,0:T(8,128)(2,1)}, bf16[512,1536]{1,0:T(8,128)(2,1)}, u32[]{:S(2)}, u32[]{:S(2)}) %collective-permute-start.17) | collective-permute-done | bytes 1572896 | tf_op jit(solution)/shard_map/ppermute | solution.py:163
  400.5 22.1 %fusion.9 = bf16[1024,1536]{1,0:T(8,128)(2,1)} fusion(bf16[1024,1536]{1,0:T(8,128)(2,1)} %copy-done.6, bf16[512,1536]{1,0:T(8,128)(2,1)} %collective-permute-done.17, bf16[512,1536]{1,0:T(8,128)(2,1)} %collective-permute-done.15, bf16[4480,1536]{1,0:T(8,128)(2,1)} %param.24, bf16[1024,4480]{1,0:T(8,128)(2,1)} %multiply_convert_fusion.clone.6), kind=kOutput, calls=%fused_computation.18 | convolution fusion | flops 14105444352 | bytes 32374784 | tf_op jit(solution)/shard_map/dot_general | solution.py:246
  (105 shorter events, 21.3 us)
Async XLA Ops:
  0.0 6.6 %copy-start = (bf16[1536,768]{1,0:T(8,128)(2,1)S(1)}, bf16[1536,768]{1,0:T(8,128)(2,1)}, u32[]{:S(2)}) copy-start(bf16[1536,768]{1,0:T(8,128)(2,1)} %param.18) | copy-start | bytes 7077892
  2.3 5.3 %copy-start.12 = (bf16[1536,256]{1,0:T(8,128)(2,1)}, bf16[1536,256]{1,0:T(8,128)(2,1)S(1)}, u32[]{:S(2)}) copy-start(bf16[1536,256]{1,0:T(8,128)(2,1)S(1)} %constant_dynamic-update-slice_fusion) | copy-start | bytes 2359300
  3.2 17.7 %collective-permute-start.2 = (bf16[768,256]{1,0:T(8,128)(2,1)}, bf16[768,256]{1,0:T(8,128)(2,1)}, u32[]{:S(2)}, u32[]{:S(2)}) collective-permute-start(bf16[768,256]{1,0:T(8,128)(2,1)} %constant_dynamic-slice_fusion.1), channel_id=1, source_target_pairs={{0,4},{4,0},{1,5},{5,1},{2,6},{6,2},{3,7},{7,3}} | collective-permute-start | bytes 1179656 | tf_op jit(solution)/shard_map/ppermute | solution.py:163
  7.7 6.6 %copy-start.15 = (bf16[1536]{0:T(1024)(128)(2,1)S(1)}, bf16[1536]{0:T(1024)(128)(2,1)}, u32[]{:S(2)}) copy-start(bf16[1536]{0:T(1024)(128)(2,1)} %param.16) | copy-start | bytes 9220
  7.7 34.1 %collective-permute-start = (bf16[768,768]{1,0:T(8,128)(2,1)}, bf16[768,768]{1,0:T(8,128)(2,1)}, u32[]{:S(2)}, u32[]{:S(2)}) collective-permute-start(bf16[768,768]{1,0:T(8,128)(2,1)} %constant_dynamic-slice_fusion.2), channel_id=1, source_target_pairs={{0,4},{4,0},{1,5},{5,1},{2,6},{6,2},{3,7},{7,3}} | collective-permute-start | bytes 3538952 | tf_op jit(solution)/shard_map/ppermute | solution.py:163
  9.0 58.1 %collective-permute-start.12 = (bf16[384,1536]{1,0:T(8,128)(2,1)S(1)}, bf16[384,1536]{1,0:T(8,128)(2,1)}, u32[]{:S(2)}, u32[]{:S(2)}) collective-permute-start(bf16[384,1536]{1,0:T(8,128)(2,1)S(1)} %constant_dynamic-slice_fusion), channel_id=1, source_target_pairs={{0,4},{4,0},{1,5},{5,1},{2,6},{6,2},{3,7},{7,3}} | collective-permute-start | bytes 3538952 | tf_op jit(solution)/shard_map/ppermute | solution.py:163
  14.2 21.9 %copy-start.13 = (f32[1536]{0:T(1024)}, f32[1536]{0:T(1024)S(1)}, u32[]{:S(2)}) copy-start(f32[1536]{0:T(1024)S(1)} %convert_element_type.82) | copy-start | bytes 18436
  16.8 4.7 %copy-start.17 = (s32[1024]{0:T(1024)S(1)}, s32[1024]{0:T(1024)}, u32[]{:S(2)}) copy-start(s32[1024]{0:T(1024)} %param.15) | copy-start | bytes 12292
  20.9 4.1 collective-permute-start.3
  25.0 3.5 copy-start.19
  28.4 2.9 copy-start.11
  31.2 4.9 %copy-start.3 = (bf16[1024,1536]{1,0:T(8,128)(2,1)S(1)}, bf16[1024,1536]{1,0:T(8,128)(2,1)}, u32[]{:S(2)}) copy-start(bf16[1024,1536]{1,0:T(8,128)(2,1)} %param.14) | copy-start | bytes 9437188
  31.2 4.9 %copy-start.18 = (f32[1024]{0:T(1024)S(1)}, f32[1024]{0:T(1024)}, u32[]{:S(2)}) copy-start(f32[1024]{0:T(1024)} %add_rsqrt_fusion.1) | copy-start | bytes 12292
  32.2 0.8 copy-start.8
  32.2 1.9 copy-start.9
  34.1 7.8 %copy-start.16 = (bf16[1536]{0:T(1024)(128)(2,1)S(1)}, bf16[1536]{0:T(1024)(128)(2,1)}, u32[]{:S(2)}) copy-start(bf16[1536]{0:T(1024)(128)(2,1)} %param.17) | copy-start | bytes 9220
  34.1 55.4 %collective-permute-start.6 = (bf16[1024,512]{1,0:T(8,128)(2,1)}, bf16[1024,512]{1,0:T(8,128)(2,1)}, u32[]{:S(2)}, u32[]{:S(2)}) collective-permute-start(bf16[1024,512]{1,0:T(8,128)(2,1)} %pad_maximum_fusion.2), channel_id=1, source_target_pairs={{0,4},{4,0},{1,5},{5,1},{2,6},{6,2},{3,7},{7,3}} | collective-permute-start | bytes 3145736 | tf_op jit(solution)/shard_map/ppermute | solution.py:163
  34.2 32.9 %collective-permute-start.4 = (bf16[1024,512]{1,0:T(8,128)(2,1)}, bf16[1024,512]{1,0:T(8,128)(2,1)}, u32[]{:S(2)}, u32[]{:S(2)}) collective-permute-start(bf16[1024,512]{1,0:T(8,128)(2,1)} %pad_maximum_fusion.2), channel_id=1, source_target_pairs={{0,2},{4,6},{1,3},{5,7},{2,0},{6,4},{3,1},{7,5}} | collective-permute-start | bytes 3145736 | tf_op jit(solution)/shard_map/ppermute | solution.py:163
  40.7 57.2 %collective-permute-start.11 = (bf16[1024,512]{1,0:T(8,128)(2,1)}, bf16[1024,512]{1,0:T(8,128)(2,1)S(1)}, u32[]{:S(2)}, u32[]{:S(2)}) collective-permute-start(bf16[1024,512]{1,0:T(8,128)(2,1)} %pad_maximum_fusion.2), channel_id=1, source_target_pairs={{0,1},{4,5},{1,0},{5,4},{2,3},{6,7},{3,2},{7,6}} | collective-permute-start | bytes 3145736 | tf_op jit(solution)/shard_map/ppermute | solution.py:163
  41.8 57.2 %collective-permute-start.1 = (bf16[768,768]{1,0:T(8,128)(2,1)}, bf16[768,768]{1,0:T(8,128)(2,1)S(1)}, u32[]{:S(2)}, u32[]{:S(2)}) collective-permute-start(bf16[768,768]{1,0:T(8,128)(2,1)} %collective-permute-done), channel_id=1, source_target_pairs={{0,1},{4,5},{1,0},{5,4},{2,3},{6,7},{3,2},{7,6}} | collective-permute-start | bytes 3538952 | tf_op jit(solution)/shard_map/ppermute | solution.py:163
  67.1 84.7 %collective-permute-start.13 = (bf16[384,1536]{1,0:T(8,128)(2,1)}, bf16[384,1536]{1,0:T(8,128)(2,1)}, u32[]{:S(2)}, u32[]{:S(2)}) collective-permute-start(bf16[384,1536]{1,0:T(8,128)(2,1)} %collective-permute-done.12), channel_id=1, source_target_pairs={{0,1},{4,5},{1,0},{5,4},{2,3},{6,7},{3,2},{7,6}} | collective-permute-start | bytes 3538952 | tf_op jit(solution)/shard_map/ppermute | solution.py:163
  69.0 40.6 %collective-permute-start.5 = (bf16[512,512]{1,0:T(8,128)(2,1)}, bf16[512,512]{1,0:T(8,128)(2,1)}, u32[]{:S(2)}, u32[]{:S(2)}) collective-permute-start(bf16[512,512]{1,0:T(8,128)(2,1)} %slice.134), channel_id=1, source_target_pairs={{0,4},{4,0},{1,5},{5,1},{2,6},{6,2},{3,7},{7,3}} | collective-permute-start | bytes 1572872 | tf_op jit(solution)/shard_map/ppermute | solution.py:163
  91.4 8.1 %copy-start.4 = (bf16[1024,1536]{1,0:T(8,128)(2,1)S(1)}, bf16[1024,1536]{1,0:T(8,128)(2,1)}, u32[]{:S(2)}) copy-start(bf16[1024,1536]{1,0:T(8,128)(2,1)} %param.14) | copy-start | bytes 9437188
  91.4 8.1 %copy-start.14 = (f32[1536]{0:T(1024)S(1)}, f32[1536]{0:T(1024)}, u32[]{:S(2)}) copy-start(f32[1536]{0:T(1024)} %copy-done.13) | copy-start | bytes 18436
  91.4 20.0 %collective-permute-start.7 = (bf16[512,512]{1,0:T(8,128)(2,1)}, bf16[512,512]{1,0:T(8,128)(2,1)}, u32[]{:S(2)}, u32[]{:S(2)}) collective-permute-start(bf16[512,512]{1,0:T(8,128)(2,1)} %slice.135), channel_id=1, source_target_pairs={{0,2},{4,6},{1,3},{5,7},{2,0},{6,4},{3,1},{7,5}} | collective-permute-start | bytes 1572872 | tf_op jit(solution)/shard_map/ppermute | solution.py:163
  97.9 57.5 %collective-permute-start.10 = (bf16[1024,512]{1,0:T(8,128)(2,1)}, bf16[1024,512]{1,0:T(8,128)(2,1)}, u32[]{:S(2)}, u32[]{:S(2)}) collective-permute-start(bf16[1024,512]{1,0:T(8,128)(2,1)} %collective-permute-done.6), channel_id=1, source_target_pairs={{0,1},{4,5},{1,0},{5,4},{2,3},{6,7},{3,2},{7,6}} | collective-permute-start | bytes 3145736 | tf_op jit(solution)/shard_map/ppermute | solution.py:163
  99.0 5.5 %copy-start.2 = (f32[1024,768]{0,1:T(8,128)S(1)}, f32[1024,768]{0,1:T(8,128)}, u32[]{:S(2)}) copy-start(f32[1024,768]{0,1:T(8,128)} %fusion.101) | copy-start | bytes 9437188
  99.0 58.7 %collective-permute-start.9 = (bf16[1024,512]{1,0:T(8,128)(2,1)}, bf16[1024,512]{1,0:T(8,128)(2,1)}, u32[]{:S(2)}, u32[]{:S(2)}) collective-permute-start(bf16[1024,512]{1,0:T(8,128)(2,1)} %collective-permute-done.4), channel_id=1, source_target_pairs={{0,1},{4,5},{1,0},{5,4},{2,3},{6,7},{3,2},{7,6}} | collective-permute-start | bytes 3145736 | tf_op jit(solution)/shard_map/ppermute | solution.py:163
  113.3 93.5 %collective-permute-start.8 = (bf16[1024,512]{1,0:T(8,128)(2,1)}, bf16[1024,512]{1,0:T(8,128)(2,1)}, u32[]{:S(2)}, u32[]{:S(2)}) collective-permute-start(bf16[1024,512]{1,0:T(8,128)(2,1)} %constant_dynamic-update-slice_fusion.2), channel_id=1, source_target_pairs={{0,1},{4,5},{1,0},{5,4},{2,3},{6,7},{3,2},{7,6}} | collective-permute-start | bytes 3145736 | tf_op jit(solution)/shard_map/ppermute | solution.py:163
  209.1 28.3 %copy-start.5 = (bf16[1024,1536]{1,0:T(8,128)(2,1)S(1)}, bf16[1024,1536]{1,0:T(8,128)(2,1)}, u32[]{:S(2)}) copy-start(bf16[1024,1536]{1,0:T(8,128)(2,1)} %param.14) | copy-start | bytes 9437188
  246.6 24.1 %copy-start.6 = (bf16[1024,1536]{1,0:T(8,128)(2,1)}, bf16[1024,1536]{1,0:T(8,128)(2,1)S(1)}, u32[]{:S(2)}) copy-start(bf16[1024,1536]{1,0:T(8,128)(2,1)S(1)} %get-tuple-element.44) | copy-start | bytes 9437188
  248.2 37.3 %collective-permute-start.14 = (bf16[512,1536]{1,0:T(8,128)(2,1)S(1)}, bf16[512,1536]{1,0:T(8,128)(2,1)S(1)}, u32[]{:S(2)}, u32[]{:S(2)}) collective-permute-start(bf16[512,1536]{1,0:T(8,128)(2,1)S(1)} %get-tuple-element.17), channel_id=1, source_target_pairs={{0,4},{4,0},{1,5},{5,1},{2,6},{6,2},{3,7},{7,3}} | collective-permute-start | bytes 4718600 | tf_op jit(solution)/shard_map/ppermute | solution.py:163
  249.7 36.1 %slice-start = ((s8[13762560]{0:T(1024)(128)(4,1)}), s8[4194304]{0:T(1024)(128)(4,1)S(1)}, s32[]{:S(2)}) async-start(s8[13762560]{0:T(1024)(128)(4,1)} %bitcast.77), calls=%async_computation | async-start | bytes 8388608
  249.7 36.1 %slice-start.1 = ((s8[13762560]{0:T(1024)(128)(4,1)}), s8[4194304]{0:T(1024)(128)(4,1)S(1)}, s32[]{:S(2)}) async-start(s8[13762560]{0:T(1024)(128)(4,1)} %bitcast.77), calls=%async_computation.1 | async-start | bytes 8388608
  249.7 36.2 %slice-start.2 = ((s8[13762560]{0:T(1024)(128)(4,1)}), s8[4194304]{0:T(1024)(128)(4,1)S(1)}, s32[]{:S(2)}) async-start(s8[13762560]{0:T(1024)(128)(4,1)} %bitcast.77), calls=%async_computation.2 | async-start | bytes 8388608
  249.7 36.2 %slice-start.3 = ((s8[13762560]{0:T(1024)(128)(4,1)}), s8[1179648]{0:T(1024)(128)(4,1)S(1)}, s32[]{:S(2)}) async-start(s8[13762560]{0:T(1024)(128)(4,1)} %bitcast.77), calls=%async_computation.3 | async-start | bytes 2359296
  249.7 74.3 %collective-permute-start.16 = (bf16[512,1536]{1,0:T(8,128)(2,1)}, bf16[512,1536]{1,0:T(8,128)(2,1)S(1)}, u32[]{:S(2)}, u32[]{:S(2)}) collective-permute-start(bf16[512,1536]{1,0:T(8,128)(2,1)} %get-tuple-element.18), channel_id=1, source_target_pairs={{0,4},{4,0},{1,5},{5,1},{2,6},{6,2},{3,7},{7,3}} | collective-permute-start | bytes 4718600 | tf_op jit(solution)/shard_map/ppermute | solution.py:163
  322.5 66.9 %collective-permute-start.15 = (bf16[512,1536]{1,0:T(8,128)(2,1)}, bf16[512,1536]{1,0:T(8,128)(2,1)}, u32[]{:S(2)}, u32[]{:S(2)}) collective-permute-start(bf16[512,1536]{1,0:T(8,128)(2,1)} %fusion.26), channel_id=1, source_target_pairs={{0,4},{4,0},{1,5},{5,1},{2,6},{6,2},{3,7},{7,3}} | collective-permute-start | bytes 4718600 | tf_op jit(solution)/shard_map/ppermute | solution.py:163
  324.0 1.1 copy-start.10
  338.3 27.5 %copy-start.7 = (bf16[1024,1536]{1,0:T(8,128)(2,1)S(1)}, bf16[1024,1536]{1,0:T(8,128)(2,1)}, u32[]{:S(2)}) copy-start(bf16[1024,1536]{1,0:T(8,128)(2,1)} %copy-done.6) | copy-start | bytes 9437188
  365.3 35.2 %collective-permute-start.17 = (bf16[512,1536]{1,0:T(8,128)(2,1)}, bf16[512,1536]{1,0:T(8,128)(2,1)}, u32[]{:S(2)}, u32[]{:S(2)}) collective-permute-start(bf16[512,1536]{1,0:T(8,128)(2,1)} %fusion.25), channel_id=1, source_target_pairs={{0,4},{4,0},{1,5},{5,1},{2,6},{6,2},{3,7},{7,3}} | collective-permute-start | bytes 4718600 | tf_op jit(solution)/shard_map/ppermute | solution.py:163
  400.5 22.1 %copy-start.1 = (bf16[1536,768]{1,0:T(8,128)(2,1)S(1)}, bf16[1536,768]{1,0:T(8,128)(2,1)}, u32[]{:S(2)}) copy-start(bf16[1536,768]{1,0:T(8,128)(2,1)} %param.18) | copy-start | bytes 7077892

commit v2 on v0

v2 whole, which is shorter than its diff:
```python
import functools
import math
import jax
import jax.numpy as jnp
import numpy as np
from jax import lax
from jax.experimental import pallas as pl
from jax.experimental.pallas import tpu as pltpu
from jax.sharding import PartitionSpec as P

DH = 128
EPS = 1e-5
THETA = 500000.0
NEG = -1e30
LC = math.log2(math.e) / math.sqrt(DH)
PC = 512
GRP = 6
D = 1536
QW = GRP * DH
FT = 896
VM = 62 * 2**20
MESH = pl.DeviceIdType.MESH


def cparams():
    return pltpu.CompilerParams(vmem_limit_bytes=VM)


def cost(flops, byts, tr=0):
    return pl.CostEstimate(flops=int(flops), bytes_accessed=int(byts), transcendentals=int(tr))


def rms(v, g):
    vf = v.astype(jnp.float32)
    inv = lax.rsqrt(jnp.mean(vf * vf, axis=-1, keepdims=True) + EPS)
    return (vf * inv * g.astype(jnp.float32)).astype(jnp.bfloat16)


def att_kernel(x_h, g_ref, cs_h, sn_h, wq_h, wk_h, wv_h, wo_h,
               h_ref, hp_ref,
               xv, csv, snv, wqb, wkb, wvb, wob, qb, kvb, m_s, al_s, acc_s, s0, s1, p0, p1, ob, hs,
               ld, ks, kr, ws, wr, hsem):
    c = lax.axis_index('cp')
    j = lax.axis_index('tp')
    core = lax.rem(c, 2)
    k = c * 2 + j
    cs_ = c + 1 - 2 * core
    cx = lax.rem(c + 2, 4)
    cxs = lax.rem(cs_ + 2, 4)
    SIB = {"cp": cs_}
    XP = {"cp": cx}
    YP = {"tp": 1 - j}
    S = [s0, s1]
    PP = [p0, p1]

    def rc(src, dst, ss, rs, dev):
        return pltpu.make_async_remote_copy(src_ref=src, dst_ref=dst, send_sem=ss, recv_sem=rs, device_id=dev, device_id_type=MESH)

    loads = [(x_h, xv), (wq_h, wqb.at[0]), (wk_h, wkb.at[0]), (wv_h, wvb.at[0]), (cs_h, csv), (sn_h, snv)]
    loads = [pltpu.make_async_copy(a, b, ld.at[i]) for i, (a, b) in enumerate(loads)]
    wol = pltpu.make_async_copy(wo_h, wob.at[pl.ds(0, QW)], ld.at[6])
    for l in loads:
        l.start()

    bar = pltpu.get_barrier_semaphore()
    for d in (SIB, XP, YP):
        pl.semaphore_signal(bar, inc=1, device_id=d, device_id_type=MESH)
    pl.semaphore_wait(bar, 3)

    wsrc = [wk_h, wv_h, wq_h, wo_h]
    wdst = [wkb.at[1], wvb.at[1], wqb.at[1], wob.at[pl.ds(QW, QW)]]

    def wcopy(i, hop):
        n = wsrc[i].shape[0] // 4
        q = c if hop < 3 else cx
        o = pl.multiple_of(q * n, n)
        dst = wdst[i].at[pl.ds(o, n)]
        src = wsrc[i].at[pl.ds(o, n)] if hop == 0 else dst
        return rc(src, dst, ws.at[i, hop], wr.at[i, hop], (YP, SIB, XP, SIB)[hop])

    def wrecv(i, hop):
        n = wsrc[i].shape[0] // 4
        q = (c, cs_, cx, cxs)[hop]
        dst = wdst[i].at[pl.ds(pl.multiple_of(q * n, n), n)]
        rc(dst, dst, ws.at[i, hop], wr.at[i, hop], (YP, SIB, XP, SIB)[hop]).wait_recv()

    KV = {'S': (0, 0, 0, 2, SIB), 'X': (0, 0, 0, 4, XP), 'Y': (0, 0, 1, 1, YP), 'XS': (0, 4, 0, 6, SIB),
          'YS': (1, 1, 1, 3, SIB), 'Z': (1, 1, 1, 5, XP), 'ZS': (1, 5, 1, 7, SIB),
          's': (1, 0, 1, 2, SIB), 'x': (1, 0, 1, 4, XP), 'y': (1, 0, 0, 1, YP), 'xs': (1, 4, 1, 6, SIB),
          'ys': (0, 1, 0, 3, SIB), 'z': (0, 1, 0, 5, XP), 'zs': (0, 5, 0, 7, SIB)}

    def kcopy(n):
        gs, ms, gd, md, dev = KV[n]
        return rc(kvb.at[gs, ms], kvb.at[gd, md], ks.at[gd, md], kr.at[gd, md], dev)

    for i in range(3):
        wcopy(i, 0).start()
    for l in loads:
        l.wait()
    wol.start()

    def front(g):
        def blk(i, _):
            r = pl.ds(pl.multiple_of(i * 256, 256), 256)
            a = rms(xv[r, :], g_ref[...])
            w = jnp.concatenate([wqb[g], wkb[g], wvb[g]], axis=1)
            y = jnp.dot(a, w, preferred_element_type=jnp.float32)
            cc = csv[r, :]
            sc = snv[r, :]
            for h in range(GRP + 1):
                u = y[:, h * DH:(h + 1) * DH]
                v = (u * cc + pltpu.roll(u, DH // 2, 1) * sc).astype(jnp.bfloat16)
                if h < GRP:
                    qb[g, r, h * DH:(h + 1) * DH] = v
                else:
                    kvb[g, 0, r, :DH] = v
            kvb[g, 0, r, DH:] = y[:, QW + DH:].astype(jnp.bfloat16)
            return 0

        lax.fori_loop(0, 4, blk, 0)

    front(0)
    for n in 'SXY':
        kcopy(n).start()

    m_s[...] = jnp.full_like(m_s, NEG)
    acc_s[...] = jnp.zeros_like(acc_s)
    al_s[...] = jnp.ones_like(al_s)
    p1[...] = jnp.zeros_like(p1)
    ones = jnp.ones((PC, 128), jnp.bfloat16)

    two = lambda g, ms: [(g, m, t) for m in ms for t in (3, 4)]
    own = lambda g: [(g, 0, 0), (g, 0, 1), (g, 0, 2)]
    last8 = [(1, 4), (1, 6), (0, 1), (0, 3), (1, 5), (1, 7), (0, 5), (0, 7)]
    seq = own(0) + two(0, (2, 4, 6)) + own(1) + two(1, (2, 1, 3)) + [(g, m, 3) for g, m in last8] + [(g, m, 4) for g, m in last8]
    NU = len(seq)
    codes = [g * 64 + m * 8 + t for g, m, t in seq]

    def code_of(u):
        v = jnp.int32(codes[0])
        for i in range(1, NU):
            v = jnp.where(u == i, codes[i], v)
        return v

    def decode(cd):
        g = cd // 64
        m = (cd // 8) % 8
        t = cd % 8
        lt = jnp.where(m >= 4, k // 4, jnp.where(m >= 2, (k // 2) % 2, k % 2))
        qp = jnp.where(t == 0, 0, jnp.where(t == 3, 1 - lt, 1))
        hf = jnp.where(t == 1, 1, jnp.where(t == 4, 1 - lt, 0))
        return g, m, t, qp, hf

    def qk(e, h):
        g, m, t, qp, hf = e
        qo = pl.multiple_of(qp * PC, PC)
        ko = pl.multiple_of(hf * PC, PC)
        S[h % 2][...] = lax.dot_general(qb[g, pl.ds(qo, PC), h * DH:(h + 1) * DH], kvb[g, m, pl.ds(ko, PC), :DH],
                                        (((1,), (1,)), ((), ())), preferred_element_type=jnp.float32)

    def sm(e, h, masked):
        g, m, t, qp, hf = e
        s = S[h % 2][...]
        if masked:
            r = lax.broadcasted_iota(jnp.int32, s.shape, 0)
            cc = lax.broadcasted_iota(jnp.int32, s.shape, 1)
            s = jnp.where(cc <= r, s, NEG)
        mx = jnp.max(s, axis=1, keepdims=True)
        mp = m_s[g, qp, h]
        mn = jnp.maximum(mp, mx)
        al_s[h % 2] = jnp.exp2((mp - mn) * LC)
        pr = jnp.exp2(s * LC - jnp.tile(mn * LC, (1, PC // 128)))
        PP[h % 2][...] = pr.astype(jnp.bfloat16)
        m_s[g, qp, h] = mn

    def pv(e, h):
        g, m, t, qp, hf = e
        ko = pl.multiple_of(hf * PC, PC)
        vb = jnp.concatenate([kvb[g, m, pl.ds(ko, PC), DH:], ones], axis=1)
        y = jnp.dot(PP[h % 2][...], vb, preferred_element_type=jnp.float32)
        acc_s[g, qp, h] = acc_s[g, qp, h] * jnp.tile(al_s[h % 2], (1, 2)) + y

    def finalize(qp):
        for g in range(2):
            for h in range(GRP):
                a = acc_s[g, qp, h]
                ob[:, (g * GRP + h) * DH:(g * GRP + h + 1) * DH] = (a[:, :128] / a[:, 128:]).astype(jnp.bfloat16)

        def blk(i, _):
            r = pl.ds(pl.multiple_of(i * 256, 256), 256)
            rx = pl.ds(pl.multiple_of(qp * PC + i * 256, 256), 256)
            y = jnp.dot(ob[r, :], wob[...], preferred_element_type=jnp.float32)
            hs[rx, :] = (xv[rx, :].astype(jnp.float32) + y).astype(jnp.bfloat16)
            return 0

        lax.fori_loop(0, 2, blk, 0)

    hcopy = rc(hs.at[pl.ds(0, PC)], hp_ref, hsem.at[0], hsem.at[1], YP)
    hout = [pltpu.make_async_copy(hs.at[pl.ds(i * PC, PC)], h_ref.at[pl.ds(i * PC, PC)], ld.at[7 + i]) for i in range(2)]

    kw = lambda n: kcopy(n).wait_recv()

    def act(u):
        def at(i):
            return pl.when(u == i)

        @at(2)
        def _():
            kw('S')

        @at(4)
        def _():
            kw('X')
            kcopy('XS').start()
            for i in range(3):
                wrecv(i, 0)
            for i in range(3):
                wcopy(i, 2).start()
                wcopy(i, 1).start()
            wcopy(3, 0).start()

        @at(6)
        def _():
            kw('XS')

        @at(8)
        def _():
            kw('Y')
            kcopy('YS').start()
            for i in range(3):
                wrecv(i, 2)
                wcopy(i, 3).start()
            kcopy('Z').start()
            for i in range(3):
                wrecv(i, 1)
            for i in range(3):
                wrecv(i, 3)
            front(1)
            for n in 'sxy':
                kcopy(n).start()

        @at(11)
        def _():
            kw('s')

        @at(13)
        def _():
            wrecv(3, 0)
            wcopy(3, 1).start()

        @at(15)
        def _():
            kw('YS')

        @at(16)
        def _():
            kw('y')
            kcopy('ys').start()
            kcopy('z').start()
            wcopy(3, 2).start()

        @at(17)
        def _():
            kw('x')
            kcopy('xs').start()
            kw('Z')
            kcopy('ZS').start()

        @at(18)
        def _():
            kw('xs')

        @at(20)
        def _():
            kw('ys')

        @at(22)
        def _():
            kw('ZS')

        @at(23)
        def _():
            kw('z')
            kcopy('zs').start()

        @at(24)
        def _():
            kw('zs')

        @at(26)
        def _():
            wrecv(3, 2)
            wcopy(3, 3).start()

        @at(27)
        def _():
            wol.wait()
            wrecv(3, 1)
            wrecv(3, 3)
            finalize(0)
            hcopy.start()
            hout[0].start()

    e0 = decode(jnp.int32(codes[0]))
    qk(e0, 0)

    def body(u, carry):
        cc, pc = carry
        act(u)
        nc = code_of(jnp.minimum(u + 1, NU - 1))
        cur, prv, nxt = decode(cc), decode(pc), decode(nc)

        def run(masked):
            for h in range(GRP):
                if h < GRP - 1:
                    qk(cur, h + 1)
                else:
                    qk(nxt, 0)
                if h == 0:
                    pv(prv, GRP - 1)
                else:
                    pv(cur, h - 1)
                sm(cur, h, masked)

        diag = cur[2] < 2

        @pl.when(diag)
        def _():
            run(True)

        @pl.when(jnp.logical_not(diag))
        def _():
            run(False)

        return nc, cc

    fin = lax.fori_loop(0, NU, body, (jnp.int32(codes[0]), jnp.int32(codes[0])))
    pv(decode(fin[1]), GRP - 1)
    finalize(1)
    hout[1].start()
    hcopy.wait_recv()
    hcopy.wait_send()
    for o in hout:
        o.wait()
    for n in KV:
        kcopy(n).wait_send()
    for i in range(4):
        for hop in range(4):
            wcopy(i, hop).wait_send()


def att(x, g, cs, sn, wq, wk, wv, wo):
    n = x.shape[0]
    any_ = pl.BlockSpec(memory_space=pl.ANY)
    vm = pl.BlockSpec(memory_space=pltpu.VMEM)
    bf, f32 = jnp.bfloat16, jnp.float32
    return pl.pallas_call(
        att_kernel,
        in_specs=[any_, vm] + [any_] * 6,
        out_specs=[any_, any_],
        out_shape=[jax.ShapeDtypeStruct((n, D), bf), jax.ShapeDtypeStruct((PC, D), bf)],
        scratch_shapes=[
            pltpu.VMEM((n, D), bf), pltpu.VMEM((n, DH), f32), pltpu.VMEM((n, DH), f32),
            pltpu.VMEM((2, D, QW), bf), pltpu.VMEM((2, D, DH), bf), pltpu.VMEM((2, D, DH), bf), pltpu.VMEM((D, D), bf),
            pltpu.VMEM((2, n, QW), bf), pltpu.VMEM((2, 8, n, 2 * DH), bf),
            pltpu.VMEM((2, 2, GRP, PC, 128), f32), pltpu.VMEM((2, PC, 128), f32), pltpu.VMEM((2, 2, GRP, PC, 256), f32),
            pltpu.VMEM((PC, PC), f32), pltpu.VMEM((PC, PC), f32), pltpu.VMEM((PC, PC), bf), pltpu.VMEM((PC, PC), bf),
            pltpu.VMEM((PC, D), bf), pltpu.VMEM((n, D), bf),
            pltpu.SemaphoreType.DMA((9,)), pltpu.SemaphoreType.DMA((2, 8)), pltpu.SemaphoreType.DMA((2, 8)),
            pltpu.SemaphoreType.DMA((4, 4)), pltpu.SemaphoreType.DMA((4, 4)), pltpu.SemaphoreType.DMA((2,))],
        compiler_params=pltpu.CompilerParams(collective_id=0, has_side_effects=True, vmem_limit_bytes=VM),
        cost_estimate=cost(70e9, 20 * 2**20), name="att")(x, g, cs, sn, wq, wk, wv, wo)


def mlp_kernel(n1, h_ref, g_ref, w1_ref, w3_ref, w2_ref, o_ref, b_s, hid_s):
    i = pl.program_id(0)

    @pl.when(i == 0)
    def _():
        b_s[...] = rms(h_ref[...], g_ref[...])

    @pl.when(i < n1)
    def _():
        w = jnp.concatenate([w1_ref[...], w3_ref[...]], axis=1)
        y = jnp.dot(b_s[...], w, preferred_element_type=jnp.float32)
        a = y[:, :FT]
        hid_s[i] = (a * jax.nn.sigmoid(a) * y[:, FT:]).astype(jnp.bfloat16)

    @pl.when(i >= n1)
    def _():
        hid = jnp.concatenate([hid_s[t] for t in range(n1)], axis=1)
        o_ref[...] = jnp.dot(hid, w2_ref[...], preferred_element_type=jnp.float32).astype(o_ref.dtype)


def mlp(h, g, w1, w3, w2, dt, name):
    n = h.shape[0]
    f = w1.shape[1]
    n1 = f // FT
    n2 = 3
    wn = D // n2
    up = pl.BlockSpec((D, FT), lambda i: (0, jnp.minimum(i, n1 - 1)))
    dn = lambda r: pl.BlockSpec((r, wn), lambda i: (0, jnp.maximum(i - n1, 0)))
    return pl.pallas_call(
        functools.partial(mlp_kernel, n1), grid=(n1 + n2,),
        in_specs=[pl.BlockSpec((n, D), lambda i: (0, 0)), pl.BlockSpec((1, D), lambda i: (0, 0)), up, up, dn(f)],
        out_specs=dn(n),
        scratch_shapes=[pltpu.VMEM((n, D), jnp.bfloat16), pltpu.VMEM((n1, n, FT), jnp.bfloat16)],
        out_shape=jax.ShapeDtypeStruct((n, D), dt),
        compiler_params=cparams(), cost_estimate=cost(6 * n * D * f, 6 * D * f), name=name)(h, g, w1, w3, w2)


def solution(mesh):
    tok = P(('dp', 'cp', 'tp'), None)
    col = P(None, 'tp')
    row = P('tp', None)
    ncp = mesh.shape['cp']
    ntp = mesh.shape['tp']

    def perm(v, dc, dj):
        pairs = []
        for c in range(ncp):
            for j in range(ntp):
                pairs.append((j * ncp + c, (j ^ dj) * ncp + (c ^ dc)))
        return lax.ppermute(v, ('tp', 'cp'), pairs)

    def local(x, pos, g1, g2, wq, wk, wv, wo, w1, w3, w2):
        freq = 1.0 / (THETA ** (jnp.arange(0, DH, 2, dtype=jnp.float32) / DH))
        ang = pos.astype(jnp.float32)[:, None] * freq
        cs = jnp.cos(ang)
        sn = jnp.sin(ang)
        cs = jnp.concatenate([cs, cs], 1)
        sn = jnp.concatenate([-sn, sn], 1)
        g2r = g2.reshape(1, D)
        h, hp_b = att(x, g1.reshape(1, D), cs, sn, wq, wk, wv, wo)
        h_b = h[:PC]
        h_a = h[PC:]
        hp_a = perm(h_a, 0, 1)
        z_b = perm(mlp(hp_b, g2r, w1, w3, w2, jnp.bfloat16, "mlp_pb"), 0, 1)
        z_a = perm(mlp(hp_a, g2r, w1, w3, w2, jnp.bfloat16, "mlp_pa"), 0, 1)
        out = []
        for hh, zr, nm in ((h_b, z_b, "mlp_ob"), (h_a, z_a, "mlp_oa")):
            z = mlp(hh, g2r, w1, w3, w2, jnp.float32, nm)
            out.append((hh.astype(jnp.float32) + (z + zr.astype(jnp.float32))).astype(jnp.bfloat16))
        return jnp.concatenate(out, 0)

    return jax.shard_map(local, mesh=mesh, in_specs=(tok, P(('dp', 'cp', 'tp')), P(None), P(None), col, col, col, row, col, col, row), out_specs=tok, check_vma=False)
```

time: 1250 us -> 313 us (0.25)
  matrix products: 528 us -> 0 us
  waiting for transfers between devices: 441 us -> 39.7 us
  Pallas kernels: 0 us -> 254 us
  other arithmetic: 232 us -> 11 us
  blocking collectives: 14.5 us -> 0 us
  between operations: 13.8 us -> 0.03 us
    dot_general x39 -> x0, matrix products: 528 us -> none  [the longest x16 194 us: blk(): o = jnp.einsum('kgqs,skd->qkgd', w, v, preferred_element_type=jnp.float32)]
    reduce_scatter x2 -> x0, waiting for transfers between devices: 283 us -> none  [the longest x1 142 us: local(): lax.psum_scatter(jnp.dot(hid, w2, preferred_element_type=jnp.float32), 't...]
    pallas_call x0 -> x5, Pallas kernels: none -> 254 us  [the longest x1 133 us: att(): pl.pallas_call(att_kernel, in_specs=[any_, vm] + [any_] * 6, out_specs=[a...]
    reduce_sum x18 -> x0, other arithmetic: 200 us -> none  [the longest x16 193 us: blk(): w = (e / jnp.sum(e, axis=-1, keepdims=True)).astype(jnp.bfloat16)]
    all_gather x4 -> x0, waiting for transfers between devices: 158 us -> none  [the longest x1 78.3 us: local(): b = lax.all_gather(rms_norm(h1, g2), 'tp', axis=0, tiled=True)]
    ppermute x0 -> x3, waiting for transfers between devices: none -> 39.7 us  [perm(): return lax.ppermute(v, ('tp', 'cp'), pairs)]
    all_gather x2 -> x0, blocking collectives: 14.5 us -> none  [the longest x1 8.84 us: local(): pa = lax.all_gather(pg, 'cp', axis=0, tiled=True)]
    while x35 -> x0, local copies, waits for them, and re-layouts: 14 us -> none  [the longest x3 13.9 us: attend(): return lax.map(blk, (qr, pr)).reshape(nq, hl * dh)]
  transfers between devices with their start and end apart: 6 -> 3, of which waited for: 5 -> 2; matrix products, arithmetic and copies ran while one was open for 2% -> 1% of each run, Pallas kernels for 0% -> 29%
where the time goes in v2:
time: 313 us
  Pallas kernels  254 us (81%)
  waiting for transfers between devices  39.7 us (13%)
  other arithmetic  11 us (4%)
  local copies, waits for them, and re-layouts  5.82 us (2%)
    pallas_call x1, Pallas kernels, att(): pl.pallas_call(att_kernel, in_specs=[any_, vm] + [any_] * 6, out_specs=[a...  133 us
    pallas_call x4, Pallas kernels, mlp(): pl.pallas_call(functools.partial(mlp_kernel, n1), grid=(n1 + n2,), in_spe...  121 us
    ppermute x3, waiting for transfers between devices, perm(): return lax.ppermute(v, ('tp', 'cp'), pairs)  39.7 us
    convert_element_type x2, other arithmetic, local(): (hh.astype(jnp.float32) + (z + zr.astype(jnp.float32))).astype(jnp.bfloat16)  7.14 us
  transfers between devices with their start and end apart: 3, of which 2 were waited for; matrix products, arithmetic and copies ran while one was open for 1% of the time, Pallas kernels for 29%

profile of v2, /device:TPU:0, one launch (start us, length us, event | category | flops | bytes accessed | tf_op | source)
XLA Modules:
  0.0 312.8 jit_solution(2473278799625940774)
XLA Ops:
  0.0 0.7 convert_element_type.21
  0.7 1.3 reshape.14.g_ref
  2.0 1.3 reshape.13.g_ref
  3.3 1.9 fusion
  5.2 1.3 pad_maximum_fusion.1
  6.5 133.0 %att.1 = (bf16[1024,1536]{1,0:T(8,128)(2,1)}, bf16[512,1536]{1,0:T(8,128)(2,1)}) custom-call(bf16[1024,1536]{1,0:T(8,128)(2,1)} %x_h.1, bf16[1,1536]{1,0:T(2,128)(2,1)} %reshape.13.g_ref, f32[1024,128]{1,0:T(8,128)} %get-tuple-element.16.cs_h, f32[1024,128]{1,0:T(8,128)} %get-tuple-element.17.sn_h, bf16[1536,768]{1,0:T(8,128)(2,1)} %wq_h.1, ...), custom_call_target="tpu_custom_call" | custom-call | flops 70000001024 | bytes 20971520 | tf_op jit(solution)/shard_map/att/pallas_call | solution.py:357
  139.5 30.2 %mlp_pb.1 = bf16[512,1536]{1,0:T(8,128)(2,1)} custom-call(bf16[512,1536]{1,0:T(8,128)(2,1)} %get-tuple-element.8.h_ref, bf16[1,1536]{1,0:T(2,128)(2,1)} %reshape.14.g_ref, bf16[1536,4480]{1,0:T(8,128)(2,1)} %w1_ref.7, bf16[1536,4480]{1,0:T(8,128)(2,1)} %w3_ref.7, bf16[4480,1536]{1,0:T(8,128)(2,1)} %w2_ref.7), custom_call_target="tpu_custom_call" | custom-call | flops 21139292160 | bytes 41287680 | tf_op jit(solution)/shard_map/mlp_pb/pallas_call | solution.py:403
  169.7 0.5 collective-permute-start
  170.2 3.3 %fusion.1 = (bf16[512,1536]{1,0:T(8,128)(2,1)}, bf16[512,1536]{1,0:T(8,128)(2,1)S(1)}) fusion(bf16[1024,1536]{1,0:T(8,128)(2,1)} %get-tuple-element.7), kind=kLoop, calls=%fused_computation.9 | loop fusion | bytes 6291456 | tf_op jit(solution)/shard_map/slice | solution.py:435
  173.5 0.0 copy-start
  173.5 1.5 collective-permute-start.1
  175.0 0.0 copy-done
  175.0 30.2 %mlp_oa.1 = f32[512,1536]{1,0:T(8,128)} custom-call(bf16[512,1536]{1,0:T(8,128)(2,1)} %copy-done, bf16[1,1536]{1,0:T(2,128)(2,1)} %reshape.14.g_ref, bf16[1536,4480]{1,0:T(8,128)(2,1)} %w1_ref.7, bf16[1536,4480]{1,0:T(8,128)(2,1)} %w3_ref.7, bf16[4480,1536]{1,0:T(8,128)(2,1)} %w2_ref.7), custom_call_target="tpu_custom_call" | custom-call | flops 21139292160 | bytes 41287680 | tf_op jit(solution)/shard_map/mlp_oa/pallas_call | solution.py:403
  205.2 34.7 %collective-permute-done.1.h_ref = bf16[512,1536]{1,0:T(8,128)(2,1)} collective-permute-done((bf16[512,1536]{1,0:T(8,128)(2,1)S(1)}, bf16[512,1536]{1,0:T(8,128)(2,1)}, u32[]{:S(2)}, u32[]{:S(2)}) %collective-permute-start.1) | collective-permute-done | bytes 1572896 | tf_op jit(solution)/shard_map/ppermute | solution.py:424
  239.9 30.0 %mlp_pa.1 = bf16[512,1536]{1,0:T(8,128)(2,1)} custom-call(bf16[512,1536]{1,0:T(8,128)(2,1)} %collective-permute-done.1.h_ref, bf16[1,1536]{1,0:T(2,128)(2,1)} %reshape.14.g_ref, bf16[1536,4480]{1,0:T(8,128)(2,1)} %w1_ref.7, bf16[1536,4480]{1,0:T(8,128)(2,1)} %w3_ref.7, bf16[4480,1536]{1,0:T(8,128)(2,1)} %w2_ref.7), custom_call_target="tpu_custom_call" | custom-call | flops 21139292160 | bytes 41287680 | tf_op jit(solution)/shard_map/mlp_pa/pallas_call | solution.py:403
  269.9 0.5 collective-permute-start.2
  270.4 30.2 %mlp_ob.1 = f32[512,1536]{1,0:T(8,128)} custom-call(bf16[512,1536]{1,0:T(8,128)(2,1)} %get-tuple-element.11.h_ref, bf16[1,1536]{1,0:T(2,128)(2,1)} %reshape.14.g_ref, bf16[1536,4480]{1,0:T(8,128)(2,1)} %w1_ref.7, bf16[1536,4480]{1,0:T(8,128)(2,1)} %w3_ref.7, bf16[4480,1536]{1,0:T(8,128)(2,1)} %w2_ref.7), custom_call_target="tpu_custom_call" | custom-call | flops 21139292160 | bytes 41287680 | tf_op jit(solution)/shard_map/mlp_ob/pallas_call | solution.py:403
  300.7 0.0 collective-permute-done
  300.7 5.0 %collective-permute-done.2 = bf16[512,1536]{1,0:T(8,128)(2,1)S(1)} collective-permute-done((bf16[512,1536]{1,0:T(8,128)(2,1)}, bf16[512,1536]{1,0:T(8,128)(2,1)S(1)}, u32[]{:S(2)}, u32[]{:S(2)}) %collective-permute-start.2) | collective-permute-done | bytes 1572896 | tf_op jit(solution)/shard_map/ppermute | solution.py:424
  305.7 7.1 %add_convert_fusion.1 = (bf16[1024,1536]{1,0:T(8,128)(2,1)}, bf16[1024,1536]{1,0:T(8,128)(2,1)}) fusion(f32[512,1536]{1,0:T(8,128)} %mlp_ob.1, bf16[512,1536]{1,0:T(8,128)(2,1)} %collective-permute-done, bf16[1024,1536]{1,0:T(8,128)(2,1)} %get-tuple-element.7, f32[512,1536]{1,0:T(8,128)} %mlp_oa.1, ...), kind=kLoop, output_to_operand_aliasing={{0}: (5, {}), {1}: (5, {})}, calls=%fused_computation.2 | loop fusion | flops 7864320 | bytes 15728640 | tf_op jit(solution)/shard_map/convert_element_type | solution.py:443
  (2 shorter events, 0.0 us)
Async XLA Ops:
  169.7 130.9 %collective-permute-start = (bf16[512,1536]{1,0:T(8,128)(2,1)}, bf16[512,1536]{1,0:T(8,128)(2,1)}, u32[]{:S(2)}, u32[]{:S(2)}) collective-permute-start(bf16[512,1536]{1,0:T(8,128)(2,1)} %mlp_pb.1), channel_id=1, source_target_pairs={{0,4},{4,0},{1,5},{5,1},{2,6},{6,2},{3,7},{7,3}} | collective-permute-start | bytes 4718600 | tf_op jit(solution)/shard_map/ppermute | solution.py:424
  173.5 1.5 copy-start
  173.5 66.4 %collective-permute-start.1 = (bf16[512,1536]{1,0:T(8,128)(2,1)S(1)}, bf16[512,1536]{1,0:T(8,128)(2,1)}, u32[]{:S(2)}, u32[]{:S(2)}) collective-permute-start(bf16[512,1536]{1,0:T(8,128)(2,1)S(1)} %get-tuple-element.12.h_ref), channel_id=1, source_target_pairs={{0,4},{4,0},{1,5},{5,1},{2,6},{6,2},{3,7},{7,3}} | collective-permute-start | bytes 4718600 | tf_op jit(solution)/shard_map/ppermute | solution.py:424
  269.9 35.7 %collective-permute-start.2 = (bf16[512,1536]{1,0:T(8,128)(2,1)}, bf16[512,1536]{1,0:T(8,128)(2,1)S(1)}, u32[]{:S(2)}, u32[]{:S(2)}) collective-permute-start(bf16[512,1536]{1,0:T(8,128)(2,1)} %mlp_pa.1), channel_id=1, source_target_pairs={{0,4},{4,0},{1,5},{5,1},{2,6},{6,2},{3,7},{7,3}} | collective-permute-start | bytes 4718600 | tf_op jit(solution)/shard_map/ppermute | solution.py:424

commit v3 on v2

--- a/solution.py
+++ b/solution.py
@@ -2,7 +2,6 @@
 import math
 import jax
 import jax.numpy as jnp
-import numpy as np
 from jax import lax
 from jax.experimental import pallas as pl
 from jax.experimental.pallas import tpu as pltpu
@@ -17,13 +16,8 @@
 GRP = 6
 D = 1536
 QW = GRP * DH
-FT = 896
 VM = 62 * 2**20
 MESH = pl.DeviceIdType.MESH
-
-
-def cparams():
-    return pltpu.CompilerParams(vmem_limit_bytes=VM)
 
 
 def cost(flops, byts, tr=0):
@@ -372,56 +366,168 @@
         cost_estimate=cost(70e9, 20 * 2**20), name="att")(x, g, cs, sn, wq, wk, wv, wo)
 
 
-def mlp_kernel(n1, h_ref, g_ref, w1_ref, w3_ref, w2_ref, o_ref, b_s, hid_s):
-    i = pl.program_id(0)
-
-    @pl.when(i == 0)
-    def _():
-        b_s[...] = rms(h_ref[...], g_ref[...])
-
-    @pl.when(i < n1)
-    def _():
-        w = jnp.concatenate([w1_ref[...], w3_ref[...]], axis=1)
-        y = jnp.dot(b_s[...], w, preferred_element_type=jnp.float32)
-        a = y[:, :FT]
-        hid_s[i] = (a * jax.nn.sigmoid(a) * y[:, FT:]).astype(jnp.bfloat16)
-
-    @pl.when(i >= n1)
-    def _():
-        hid = jnp.concatenate([hid_s[t] for t in range(n1)], axis=1)
-        o_ref[...] = jnp.dot(hid, w2_ref[...], preferred_element_type=jnp.float32).astype(o_ref.dtype)
-
-
-def mlp(h, g, w1, w3, w2, dt, name):
+FU = 640
+ND = 512
+
+
+def mlp_kernel(h_h, hpb_h, g_ref, w1_h, w3_h, w2_h, o_h, hall, wb, w2b, hid, b_s, zs, zr, zo, ld, us, ds, zsem, zrm):
+    j = lax.axis_index('tp')
+    YP = {"tp": 1 - j}
+    F = w1_h.shape[1]
+    NU_, NDN = F // FU, D // ND
+
+    def rc(src, dst, ss, rs):
+        return pltpu.make_async_remote_copy(src_ref=src, dst_ref=dst, send_sem=ss, recv_sem=rs, device_id=YP, device_id_type=MESH)
+
+    def up(t, slot):
+        o = pl.multiple_of(t * FU, 128)
+        return [pltpu.make_async_copy(w1_h.at[:, pl.ds(o, FU)], wb.at[slot, :, pl.ds(0, FU)], us.at[slot, 0]),
+                pltpu.make_async_copy(w3_h.at[:, pl.ds(o, FU)], wb.at[slot, :, pl.ds(FU, FU)], us.at[slot, 1])]
+
+    def down(t, slot):
+        return pltpu.make_async_copy(w2_h.at[:, pl.ds(pl.multiple_of(t * ND, 128), ND)], w2b.at[slot], ds.at[slot])
+
+    hl = [pltpu.make_async_copy(hpb_h, hall.at[2], ld.at[0]),
+          pltpu.make_async_copy(h_h.at[pl.ds(0, PC)], hall.at[0], ld.at[1]),
+          pltpu.make_async_copy(h_h.at[pl.ds(PC, PC)], hall.at[1], ld.at[2])]
+    hl[0].start()
+    for cp in up(0, 0):
+        cp.start()
+    for cp in hl[1:]:
+        cp.start()
+
+    bar = pltpu.get_barrier_semaphore()
+    pl.semaphore_signal(bar, inc=1, device_id=YP, device_id_type=MESH)
+    pl.semaphore_wait(bar, 1)
+    hsend = rc(h_h.at[pl.ds(PC, PC)], hall.at[3], zsem.at[2], zrm.at[2])
+    hsend.start()
+    zc = [rc(zs.at[i], zr.at[i], zsem.at[i], zrm.at[i]) for i in range(2)]
+    oc = [pltpu.make_async_copy(hall.at[i], o_h.at[pl.ds(i * PC, PC)], ld.at[3 + i]) for i in range(2)]
+
+    def finish(i):
+        zc[i].wait_recv()
+
+        def blk(t, _):
+            r = pl.ds(pl.multiple_of(t * 128, 128), 128)
+            y = hall[i, r, :].astype(jnp.float32) + (zo[i, r, :] + zr[i, r, :].astype(jnp.float32))
+            hall[i, r, :] = y.astype(jnp.bfloat16)
+            return 0
+
+        lax.fori_loop(0, PC // 128, blk, 0)
+        oc[i].start()
+
+    def chunk(ci, _):
+        peer = ci % 2 == 0
+        half = ci // 2
+        idx = jnp.where(peer, 2, 0) + half
+
+        @pl.when(ci == 0)
+        def _():
+            hl[0].wait()
+
+        @pl.when(ci == 1)
+        def _():
+            hl[1].wait()
+
+        @pl.when(ci == 2)
+        def _():
+            hsend.wait_recv()
+
+        @pl.when(ci == 3)
+        def _():
+            hl[2].wait()
+
+        b_s[...] = rms(hall[idx], g_ref[...])
+
+        @pl.when(ci == 1)
+        def _():
+            zc[0].start()
+
+        @pl.when(ci == 3)
+        def _():
+            zc[1].start()
+            finish(0)
+
+        def ustep(t, _):
+            n = ci * NU_ + t
+            slot = n % 2
+            last = t == NU_ - 1
+
+            @pl.when(jnp.logical_not(jnp.logical_and(last, ci == 3)))
+            def _():
+                for cp in up(jnp.where(last, 0, t + 1), 1 - slot):
+                    cp.start()
+
+            @pl.when(t == NU_ - 2)
+            def _():
+                down(0, (ci * NDN) % 2).start()
+
+            for cp in up(t, slot):
+                cp.wait()
+            y = jnp.dot(b_s[...], wb[slot], preferred_element_type=jnp.float32)
+            a = y[:, :FU]
+            hid[:, pl.ds(pl.multiple_of(t * FU, 128), FU)] = (a * jax.nn.sigmoid(a) * y[:, FU:]).astype(jnp.bfloat16)
+            return 0
+
+        lax.fori_loop(0, NU_, ustep, 0)
+
+        def dstep(t, _):
+            n = ci * NDN + t
+            slot = n % 2
+
+            @pl.when(t < NDN - 1)
+            def _():
+                down(t + 1, 1 - slot).start()
+
+            down(t, slot).wait()
+            y = jnp.dot(hid[...], w2b[slot], preferred_element_type=jnp.float32)
+            cols = pl.ds(pl.multiple_of(t * ND, 128), ND)
+
+            @pl.when(peer)
+            def _():
+                zs[half, :, cols] = y.astype(jnp.bfloat16)
+
+            @pl.when(jnp.logical_not(peer))
+            def _():
+                zo[half, :, cols] = y
+
+            return 0
+
+        lax.fori_loop(0, NDN, dstep, 0)
+        return 0
+
+    lax.fori_loop(0, 4, chunk, 0)
+    finish(1)
+    hsend.wait_send()
+    for i in range(2):
+        zc[i].wait_send()
+        oc[i].wait()
+
+
+def mlp(h, hpb, g, w1, w3, w2):
     n = h.shape[0]
     f = w1.shape[1]
-    n1 = f // FT
-    n2 = 3
-    wn = D // n2
-    up = pl.BlockSpec((D, FT), lambda i: (0, jnp.minimum(i, n1 - 1)))
-    dn = lambda r: pl.BlockSpec((r, wn), lambda i: (0, jnp.maximum(i - n1, 0)))
+    any_ = pl.BlockSpec(memory_space=pl.ANY)
+    bf, f32 = jnp.bfloat16, jnp.float32
     return pl.pallas_call(
-        functools.partial(mlp_kernel, n1), grid=(n1 + n2,),
-        in_specs=[pl.BlockSpec((n, D), lambda i: (0, 0)), pl.BlockSpec((1, D), lambda i: (0, 0)), up, up, dn(f)],
-        out_specs=dn(n),
-        scratch_shapes=[pltpu.VMEM((n, D), jnp.bfloat16), pltpu.VMEM((n1, n, FT), jnp.bfloat16)],
-        out_shape=jax.ShapeDtypeStruct((n, D), dt),
-        compiler_params=cparams(), cost_estimate=cost(6 * n * D * f, 6 * D * f), name=name)(h, g, w1, w3, w2)
+        mlp_kernel,
+        in_specs=[any_, any_, pl.BlockSpec(memory_space=pltpu.VMEM), any_, any_, any_],
+        out_specs=any_,
+        out_shape=jax.ShapeDtypeStruct((n, D), bf),
+        scratch_shapes=[
+            pltpu.VMEM((4, PC, D), bf), pltpu.VMEM((2, D, 2 * FU), bf), pltpu.VMEM((2, f, ND), bf),
+            pltpu.VMEM((PC, f), bf), pltpu.VMEM((PC, D), bf), pltpu.VMEM((2, PC, D), bf), pltpu.VMEM((2, PC, D), bf),
+            pltpu.VMEM((2, PC, D), f32),
+            pltpu.SemaphoreType.DMA((5,)), pltpu.SemaphoreType.DMA((2, 2)), pltpu.SemaphoreType.DMA((2,)),
+            pltpu.SemaphoreType.DMA((3,)), pltpu.SemaphoreType.DMA((3,))],
+        compiler_params=pltpu.CompilerParams(collective_id=1, has_side_effects=True, vmem_limit_bytes=VM),
+        cost_estimate=cost(12 * n * D * f, 24 * D * f), name="mlp")(h, hpb, g, w1, w3, w2)
 
 
 def solution(mesh):
     tok = P(('dp', 'cp', 'tp'), None)
     col = P(None, 'tp')
     row = P('tp', None)
-    ncp = mesh.shape['cp']
-    ntp = mesh.shape['tp']
-
-    def perm(v, dc, dj):
-        pairs = []
-        for c in range(ncp):
-            for j in range(ntp):
-                pairs.append((j * ncp + c, (j ^ dj) * ncp + (c ^ dc)))
-        return lax.ppermute(v, ('tp', 'cp'), pairs)
 
     def local(x, pos, g1, g2, wq, wk, wv, wo, w1, w3, w2):
         freq = 1.0 / (THETA ** (jnp.arange(0, DH, 2, dtype=jnp.float32) / DH))
@@ -430,17 +536,7 @@
         sn = jnp.sin(ang)
         cs = jnp.concatenate([cs, cs], 1)
         sn = jnp.concatenate([-sn, sn], 1)
-        g2r = g2.reshape(1, D)
-        h, hp_b = att(x, g1.reshape(1, D), cs, sn, wq, wk, wv, wo)
-        h_b = h[:PC]
-        h_a = h[PC:]
-        hp_a = perm(h_a, 0, 1)
-        z_b = perm(mlp(hp_b, g2r, w1, w3, w2, jnp.bfloat16, "mlp_pb"), 0, 1)
-        z_a = perm(mlp(hp_a, g2r, w1, w3, w2, jnp.bfloat16, "mlp_pa"), 0, 1)
-        out = []
-        for hh, zr, nm in ((h_b, z_b, "mlp_ob"), (h_a, z_a, "mlp_oa")):
-            z = mlp(hh, g2r, w1, w3, w2, jnp.float32, nm)
-            out.append((hh.astype(jnp.float32) + (z + zr.astype(jnp.float32))).astype(jnp.bfloat16))
-        return jnp.concatenate(out, 0)
+        h, hp = att(x, g1.reshape(1, D), cs, sn, wq, wk, wv, wo)
+        return mlp(h, hp, g2.reshape(1, D), w1, w3, w2)
 
     return jax.shard_map(local, mesh=mesh, in_specs=(tok, P(('dp', 'cp', 'tp')), P(None), P(None), col, col, col, row, col, col, row), out_specs=tok, check_vma=False)

time: 313 us -> 257 us (0.82)
  waiting for transfers between devices: 39.7 us -> 0 us
  Pallas kernels: 254 us -> 246 us
  other arithmetic: 11 us -> 3.91 us
    ppermute x3 -> x0, waiting for transfers between devices: 39.7 us -> none  [perm(): return lax.ppermute(v, ('tp', 'cp'), pairs)]
    pallas_call x4 -> x1, Pallas kernels: 121 us -> 113 us  [mlp(): pl.pallas_call(mlp_kernel, in_specs=[any_, any_, pl.BlockSpec(memory_spac...]
    convert_element_type x2 -> x0, other arithmetic: 7.14 us -> none  [local(): (hh.astype(jnp.float32) + (z + zr.astype(jnp.float32))).astype(jnp.bfloat16)]
    unnamed x2 -> x1, local copies, waits for them, and re-layouts: 0.01 us -> 3.76 us
    slice x1 -> x0, local copies, waits for them, and re-layouts: 3.26 us -> none  [local(): h_b = h[:PC]]
  transfers between devices with their start and end apart: 3 -> 0, of which waited for: 2 -> 0; matrix products, arithmetic and copies ran while one was open for 1% -> 0% of each run, Pallas kernels for 29% -> 0%
where the time goes in v3:
time: 257 us; the launch traced here: 256 us
  Pallas kernels  246 us (96%)
  local copies, waits for them, and re-layouts  6.32 us (2%)
  other arithmetic  3.91 us (2%)
    pallas_call x1, Pallas kernels, att(): pl.pallas_call(att_kernel, in_specs=[any_, vm] + [any_] * 6, out_specs=[a...  133 us
    pallas_call x1, Pallas kernels, mlp(): pl.pallas_call(mlp_kernel, in_specs=[any_, any_, pl.BlockSpec(memory_spac...  113 us

profile of v3, /device:TPU:0, one launch (start us, length us, event | category | flops | bytes accessed | tf_op | source)
XLA Modules:
  0.0 256.4 jit_solution(14038390013695134537)
XLA Ops:
  0.0 0.7 convert_element_type.3
  0.7 1.3 reshape.13.g_ref
  2.0 1.3 reshape.14.g_ref
  3.3 1.9 fusion
  5.2 1.3 pad_maximum_fusion
  6.5 133.0 %att.1 = (bf16[1024,1536]{1,0:T(8,128)(2,1)}, bf16[512,1536]{1,0:T(8,128)(2,1)}) custom-call(bf16[1024,1536]{1,0:T(8,128)(2,1)} %x_h.1, bf16[1,1536]{1,0:T(2,128)(2,1)} %reshape.13.g_ref, f32[1024,128]{1,0:T(8,128)} %get-tuple-element.12.cs_h, f32[1024,128]{1,0:T(8,128)} %get-tuple-element.13.sn_h, bf16[1536,768]{1,0:T(8,128)(2,1)} %wq_h.1, ...), custom_call_target="tpu_custom_call" | custom-call | flops 70000001024 | bytes 20971520 | tf_op jit(solution)/shard_map/att/pallas_call | solution.py:351
  139.5 113.1 %mlp.1 = bf16[1024,1536]{1,0:T(8,128)(2,1)} custom-call(bf16[1024,1536]{1,0:T(8,128)(2,1)} %get-tuple-element.7.h_h, bf16[512,1536]{1,0:T(8,128)(2,1)} %get-tuple-element.8.hpb_h, bf16[1,1536]{1,0:T(2,128)(2,1)} %reshape.14.g_ref, bf16[1536,4480]{1,0:T(8,128)(2,1)} %w1_h.1, bf16[1536,4480]{1,0:T(8,128)(2,1)} %w3_h.1, bf16[4480,1536]{1,0:T(8,128)(2,1)} %w2_h.1), custom_call_target="tpu_custom_call" | custom-call | flops 84557168640 | bytes 165150720 | tf_op jit(solution)/shard_map/mlp/pallas_call | solution.py:512
  252.7 3.8 %copy.13 = bf16[1024,1536]{1,0:T(8,128)(2,1)} copy(bf16[1024,1536]{1,0:T(8,128)(2,1)} %mlp.1) | data formatting | bytes 6291456
  (1 shorter events, 0.0 us)

commit v4 on v3

--- a/solution.py
+++ b/solution.py
@@ -61,22 +61,28 @@
         pl.semaphore_signal(bar, inc=1, device_id=d, device_id_type=MESH)
     pl.semaphore_wait(bar, 3)
 
-    wsrc = [wk_h, wv_h, wq_h, wo_h]
-    wdst = [wkb.at[1], wvb.at[1], wqb.at[1], wob.at[pl.ds(QW, QW)]]
-
-    def wcopy(i, hop):
-        n = wsrc[i].shape[0] // 4
-        q = c if hop < 3 else cx
-        o = pl.multiple_of(q * n, n)
-        dst = wdst[i].at[pl.ds(o, n)]
-        src = wsrc[i].at[pl.ds(o, n)] if hop == 0 else dst
-        return rc(src, dst, ws.at[i, hop], wr.at[i, hop], (YP, SIB, XP, SIB)[hop])
-
-    def wrecv(i, hop):
-        n = wsrc[i].shape[0] // 4
-        q = (c, cs_, cx, cxs)[hop]
-        dst = wdst[i].at[pl.ds(pl.multiple_of(q * n, n), n)]
-        rc(dst, dst, ws.at[i, hop], wr.at[i, hop], (YP, SIB, XP, SIB)[hop]).wait_recv()
+    W = {'k': (wk_h, wkb.at[1], 2, 0, 1), 'v': (wv_h, wvb.at[1], 2, 0, 1), 'qa': (wq_h, wqb.at[1], 4, 0, 2),
+         'qb': (wq_h, wqb.at[1], 4, 1, 2), 'o': (wo_h, wob.at[pl.ds(QW, QW)], 2, 0, 1)}
+    WI = {n: i for i, n in enumerate(W)}
+
+    def wrange(n, q):
+        src, dst, div, sub, nsub = W[n]
+        r = src.shape[0] // div
+        return pl.ds(pl.multiple_of(q * r + sub * (r // nsub), r // nsub), r // nsub)
+
+    def wcopy(n, hop):
+        src, dst, div, sub, nsub = W[n]
+        q = core if div == 2 else (c if hop < 3 else cx)
+        rg = wrange(n, q)
+        i = WI[n]
+        return rc((src if hop == 0 else dst).at[rg], dst.at[rg], ws.at[i, hop], wr.at[i, hop], (YP, SIB, XP, SIB)[hop])
+
+    def wrecv(n, hop):
+        src, dst, div, sub, nsub = W[n]
+        q = (core, 1 - core)[hop] if div == 2 else (c, cs_, cx, cxs)[hop]
+        rg = wrange(n, q)
+        i = WI[n]
+        rc(dst.at[rg], dst.at[rg], ws.at[i, hop], wr.at[i, hop], (YP, SIB, XP, SIB)[hop]).wait_recv()
 
     KV = {'S': (0, 0, 0, 2, SIB), 'X': (0, 0, 0, 4, XP), 'Y': (0, 0, 1, 1, YP), 'XS': (0, 4, 0, 6, SIB),
           'YS': (1, 1, 1, 3, SIB), 'Z': (1, 1, 1, 5, XP), 'ZS': (1, 5, 1, 7, SIB),
@@ -87,34 +93,38 @@
         gs, ms, gd, md, dev = KV[n]
         return rc(kvb.at[gs, ms], kvb.at[gd, md], ks.at[gd, md], kr.at[gd, md], dev)
 
-    for i in range(3):
-        wcopy(i, 0).start()
+    for n in ('k', 'v', 'qa'):
+        wcopy(n, 0).start()
     for l in loads:
         l.wait()
     wol.start()
 
-    def front(g):
+    def front(g, do_q, do_kv):
         def blk(i, _):
             r = pl.ds(pl.multiple_of(i * 256, 256), 256)
-            a = rms(xv[r, :], g_ref[...])
-            w = jnp.concatenate([wqb[g], wkb[g], wvb[g]], axis=1)
-            y = jnp.dot(a, w, preferred_element_type=jnp.float32)
+            a = rms(xv[r, :], g_ref[0:1, :])
+            ww = ([wqb[g]] if do_q else []) + ([wkb[g], wvb[g]] if do_kv else [])
+            y = jnp.dot(a, jnp.concatenate(ww, axis=1) if len(ww) > 1 else ww[0], preferred_element_type=jnp.float32)
             cc = csv[r, :]
             sc = snv[r, :]
-            for h in range(GRP + 1):
+
+            def rot(h):
                 u = y[:, h * DH:(h + 1) * DH]
-                v = (u * cc + pltpu.roll(u, DH // 2, 1) * sc).astype(jnp.bfloat16)
-                if h < GRP:
-                    qb[g, r, h * DH:(h + 1) * DH] = v
-                else:
-                    kvb[g, 0, r, :DH] = v
-            kvb[g, 0, r, DH:] = y[:, QW + DH:].astype(jnp.bfloat16)
+                return (u * cc + pltpu.roll(u, DH // 2, 1) * sc).astype(jnp.bfloat16)
+
+            if do_q:
+                for h in range(GRP):
+                    qb[g, r, h * DH:(h + 1) * DH] = rot(h)
+            if do_kv:
+                n = GRP if do_q else 0
+                kvb[g, 0, r, :DH] = rot(n)
+                kvb[g, 0, r, DH:] = y[:, (n + 1) * DH:(n + 2) * DH].astype(jnp.bfloat16)
             return 0
 
         lax.fori_loop(0, 4, blk, 0)
 
-    front(0)
-    for n in 'SXY':
+    front(0, True, True)
+    for n in 'SX':
         kcopy(n).start()
 
     m_s[...] = jnp.full_like(m_s, NEG)
@@ -124,9 +134,9 @@
     ones = jnp.ones((PC, 128), jnp.bfloat16)
 
     two = lambda g, ms: [(g, m, t) for m in ms for t in (3, 4)]
-    own = lambda g: [(g, 0, 0), (g, 0, 1), (g, 0, 2)]
-    last8 = [(1, 4), (1, 6), (0, 1), (0, 3), (1, 5), (1, 7), (0, 5), (0, 7)]
-    seq = own(0) + two(0, (2, 4, 6)) + own(1) + two(1, (2, 1, 3)) + [(g, m, 3) for g, m in last8] + [(g, m, 4) for g, m in last8]
+    late = (2, 1, 3, 4, 6, 5, 7)
+    seq = [(0, 0, 0), (0, 0, 1), (0, 0, 2)] + two(0, (2, 4, 6, 1, 3, 5, 7)) + [(1, 0, 0)] + [(1, m, 3) for m in late]
+    seq = seq + [(1, 0, 1), (1, 0, 2)] + [(1, m, 4) for m in late]
     NU = len(seq)
     codes = [g * 64 + m * 8 + t for g, m, t in seq]
 
@@ -200,97 +210,109 @@
 
         @at(2)
         def _():
+            for n in 'kv':
+                wrecv(n, 0)
+                wcopy(n, 1).start()
             kw('S')
+
+        @at(3)
+        def _():
+            for n in 'kv':
+                wrecv(n, 1)
+            front(1, False, True)
+            kcopy('s').start()
+            kcopy('y').start()
+            wcopy('qb', 0).start()
+            kcopy('Y').start()
 
         @at(4)
         def _():
             kw('X')
             kcopy('XS').start()
-            for i in range(3):
-                wrecv(i, 0)
-            for i in range(3):
-                wcopy(i, 2).start()
-                wcopy(i, 1).start()
-            wcopy(3, 0).start()
+            wrecv('qa', 0)
+            wcopy('qa', 2).start()
+            wcopy('qa', 1).start()
 
         @at(6)
         def _():
             kw('XS')
 
         @at(8)
-        def _():
-            kw('Y')
-            kcopy('YS').start()
-            for i in range(3):
-                wrecv(i, 2)
-                wcopy(i, 3).start()
-            kcopy('Z').start()
-            for i in range(3):
-                wrecv(i, 1)
-            for i in range(3):
-                wrecv(i, 3)
-            front(1)
-            for n in 'sxy':
-                kcopy(n).start()
-
-        @at(11)
-        def _():
-            kw('s')
-
-        @at(13)
-        def _():
-            wrecv(3, 0)
-            wcopy(3, 1).start()
-
-        @at(15)
-        def _():
-            kw('YS')
-
-        @at(16)
         def _():
             kw('y')
             kcopy('ys').start()
             kcopy('z').start()
-            wcopy(3, 2).start()
-
-        @at(17)
+
+        @at(10)
+        def _():
+            kw('ys')
+
+        @at(11)
+        def _():
+            wrecv('qb', 0)
+            wcopy('qb', 2).start()
+            wcopy('qb', 1).start()
+            kcopy('x').start()
+            wcopy('o', 0).start()
+
+        @at(12)
+        def _():
+            kw('z')
+            kcopy('zs').start()
+
+        @at(14)
+        def _():
+            kw('zs')
+            wrecv('qa', 2)
+            wcopy('qa', 3).start()
+
+        @at(15)
+        def _():
+            kw('Y')
+            kcopy('YS').start()
+            kcopy('Z').start()
+
+        @at(16)
+        def _():
+            wrecv('qb', 2)
+            wcopy('qb', 3).start()
+            kw('s')
+            for n in ('qa', 'qb'):
+                wrecv(n, 1)
+                wrecv(n, 3)
+            front(1, True, False)
+
+        @at(19)
+        def _():
+            kw('YS')
+
+        @at(20)
         def _():
             kw('x')
             kcopy('xs').start()
+
+        @at(21)
+        def _():
+            kw('xs')
+
+        @at(22)
+        def _():
             kw('Z')
             kcopy('ZS').start()
 
-        @at(18)
-        def _():
-            kw('xs')
-
-        @at(20)
-        def _():
-            kw('ys')
-
-        @at(22)
+        @at(23)
         def _():
             kw('ZS')
 
-        @at(23)
-        def _():
-            kw('z')
-            kcopy('zs').start()
-
         @at(24)
         def _():
-            kw('zs')
+            wrecv('o', 0)
+            wcopy('o', 1).start()
 
         @at(26)
         def _():
-            wrecv(3, 2)
-            wcopy(3, 3).start()
-
-        @at(27)
-        def _():
             wol.wait()
-            wrecv(3, 1)
-            wrecv(3, 3)
+            wrecv('o', 1)
             finalize(0)
             hcopy.start()
             hout[0].start()
@@ -338,9 +360,9 @@
         o.wait()
     for n in KV:
         kcopy(n).wait_send()
-    for i in range(4):
-        for hop in range(4):
-            wcopy(i, hop).wait_send()
+    for n in W:
+        for hop in range(W[n][2]):
+            wcopy(n, hop).wait_send()
 
 
 def att(x, g, cs, sn, wq, wk, wv, wo):
@@ -361,13 +383,13 @@
             pltpu.VMEM((PC, PC), f32), pltpu.VMEM((PC, PC), f32), pltpu.VMEM((PC, PC), bf), pltpu.VMEM((PC, PC), bf),
             pltpu.VMEM((PC, D), bf), pltpu.VMEM((n, D), bf),
             pltpu.SemaphoreType.DMA((9,)), pltpu.SemaphoreType.DMA((2, 8)), pltpu.SemaphoreType.DMA((2, 8)),
-            pltpu.SemaphoreType.DMA((4, 4)), pltpu.SemaphoreType.DMA((4, 4)), pltpu.SemaphoreType.DMA((2,))],
+            pltpu.SemaphoreType.DMA((5, 4)), pltpu.SemaphoreType.DMA((5, 4)), pltpu.SemaphoreType.DMA((2,))],
         compiler_params=pltpu.CompilerParams(collective_id=0, has_side_effects=True, vmem_limit_bytes=VM),
         cost_estimate=cost(70e9, 20 * 2**20), name="att")(x, g, cs, sn, wq, wk, wv, wo)
 
 
-FU = 640
-ND = 512
+FU = 896
+ND = 768
 
 
 def mlp_kernel(h_h, hpb_h, g_ref, w1_h, w3_h, w2_h, o_h, hall, wb, w2b, hid, b_s, zs, zr, zo, ld, us, ds, zsem, zrm):
@@ -416,87 +438,66 @@
         lax.fori_loop(0, PC // 128, blk, 0)
         oc[i].start()
 
-    def chunk(ci, _):
-        peer = ci % 2 == 0
-        half = ci // 2
-        idx = jnp.where(peer, 2, 0) + half
-
-        @pl.when(ci == 0)
-        def _():
-            hl[0].wait()
-
-        @pl.when(ci == 1)
-        def _():
-            hl[1].wait()
-
-        @pl.when(ci == 2)
-        def _():
-            hsend.wait_recv()
-
-        @pl.when(ci == 3)
-        def _():
-            hl[2].wait()
-
-        b_s[...] = rms(hall[idx], g_ref[...])
-
-        @pl.when(ci == 1)
-        def _():
-            zc[0].start()
-
-        @pl.when(ci == 3)
-        def _():
-            zc[1].start()
-            finish(0)
-
-        def ustep(t, _):
-            n = ci * NU_ + t
-            slot = n % 2
+    def up_phase(n, idx, hb, more, pre):
+        b_s[...] = rms(hall[idx], g_ref[1:2, :])
+
+        def step(t, _):
+            slot = (n * NU_ + t) % 2
             last = t == NU_ - 1
 
-            @pl.when(jnp.logical_not(jnp.logical_and(last, ci == 3)))
+            @pl.when(jnp.logical_or(more, jnp.logical_not(last)))
             def _():
                 for cp in up(jnp.where(last, 0, t + 1), 1 - slot):
                     cp.start()
 
-            @pl.when(t == NU_ - 2)
-            def _():
-                down(0, (ci * NDN) % 2).start()
+            if pre is not None:
+                @pl.when(t == NU_ - 2)
+                def _():
+                    down(0, pre).start()
 
             for cp in up(t, slot):
                 cp.wait()
             y = jnp.dot(b_s[...], wb[slot], preferred_element_type=jnp.float32)
             a = y[:, :FU]
-            hid[:, pl.ds(pl.multiple_of(t * FU, 128), FU)] = (a * jax.nn.sigmoid(a) * y[:, FU:]).astype(jnp.bfloat16)
+            hid[hb, :, pl.ds(pl.multiple_of(t * FU, 128), FU)] = (a * jax.nn.sigmoid(a) * y[:, FU:]).astype(jnp.bfloat16)
             return 0
 
-        lax.fori_loop(0, NU_, ustep, 0)
-
-        def dstep(t, _):
-            n = ci * NDN + t
-            slot = n % 2
-
-            @pl.when(t < NDN - 1)
+        lax.fori_loop(0, NU_, step, 0)
+
+    def down_phase(n, idx, hb, chain):
+        def step(t, _):
+            slot = (n * NDN + t) % 2
+
+            @pl.when(jnp.logical_or(chain, t < NDN - 1))
             def _():
-                down(t + 1, 1 - slot).start()
+                down(jnp.where(t == NDN - 1, 0, t + 1), 1 - slot).start()
 
             down(t, slot).wait()
-            y = jnp.dot(hid[...], w2b[slot], preferred_element_type=jnp.float32)
+            y = jnp.dot(hid[hb], w2b[slot], preferred_element_type=jnp.float32)
             cols = pl.ds(pl.multiple_of(t * ND, 128), ND)
-
-            @pl.when(peer)
-            def _():
-                zs[half, :, cols] = y.astype(jnp.bfloat16)
-
-            @pl.when(jnp.logical_not(peer))
-            def _():
-                zo[half, :, cols] = y
-
+            if idx >= 2:
+                zs[idx - 2, :, cols] = y.astype(jnp.bfloat16)
+            else:
+                zo[idx, :, cols] = y
             return 0
 
-        lax.fori_loop(0, NDN, dstep, 0)
-        return 0
-
-    lax.fori_loop(0, 4, chunk, 0)
+        lax.fori_loop(0, NDN, step, 0)
+
+    hl[0].wait()
+    up_phase(0, 2, 0, True, 0)
+    down_phase(0, 2, 0, False)
+    hl[1].wait()
+    zc[0].start()
+    up_phase(1, 0, 1, True, None)
+    hsend.wait_recv()
+    up_phase(2, 3, 0, True, NDN % 2)
+    down_phase(1, 3, 0, True)
+    hl[2].wait()
+    zc[1].start()
+    down_phase(2, 0, 1, False)
+    finish(0)
+    up_phase(3, 1, 0, False, (3 * NDN) % 2)
+    down_phase(3, 1, 0, False)
     finish(1)
     hsend.wait_send()
     for i in range(2):
@@ -516,7 +517,7 @@
         out_shape=jax.ShapeDtypeStruct((n, D), bf),
         scratch_shapes=[
             pltpu.VMEM((4, PC, D), bf), pltpu.VMEM((2, D, 2 * FU), bf), pltpu.VMEM((2, f, ND), bf),
-            pltpu.VMEM((PC, f), bf), pltpu.VMEM((PC, D), bf), pltpu.VMEM((2, PC, D), bf), pltpu.VMEM((2, PC, D), bf),
+            pltpu.VMEM((2, PC, f), bf), pltpu.VMEM((PC, D), bf), pltpu.VMEM((2, PC, D), bf), pltpu.VMEM((2, PC, D), bf),
             pltpu.VMEM((2, PC, D), f32),
             pltpu.SemaphoreType.DMA((5,)), pltpu.SemaphoreType.DMA((2, 2)), pltpu.SemaphoreType.DMA((2,)),
             pltpu.SemaphoreType.DMA((3,)), pltpu.SemaphoreType.DMA((3,))],
@@ -536,7 +537,8 @@
         sn = jnp.sin(ang)
         cs = jnp.concatenate([cs, cs], 1)
         sn = jnp.concatenate([-sn, sn], 1)
-        h, hp = att(x, g1.reshape(1, D), cs, sn, wq, wk, wv, wo)
-        return mlp(h, hp, g2.reshape(1, D), w1, w3, w2)
+        gs = jnp.stack([g1, g2])
+        h, hp = att(x, gs, cs, sn, wq, wk, wv, wo)
+        return mlp(h, hp, gs, w1, w3, w2)
 
     return jax.shard_map(local, mesh=mesh, in_specs=(tok, P(('dp', 'cp', 'tp')), P(None), P(None), col, col, col, row, col, col, row), out_specs=tok, check_vma=False)

time: 257 us -> 241 us (0.938)
  Pallas kernels: 246 us -> 231 us
    pallas_call x1, Pallas kernels: 133 us -> 125 us  [att(): pl.pallas_call(att_kernel, in_specs=[any_, vm] + [any_] * 6, out_specs=[a...]
    pallas_call x1, Pallas kernels: 113 us -> 106 us  [mlp(): pl.pallas_call(mlp_kernel, in_specs=[any_, any_, pl.BlockSpec(memory_spac...]
where the time goes in v4:
time: 241 us
  Pallas kernels  231 us (96%)
  local copies, waits for them, and re-layouts  5.14 us (2%)
  other arithmetic  4.51 us (2%)
    pallas_call x1, Pallas kernels, att(): pl.pallas_call(att_kernel, in_specs=[any_, vm] + [any_] * 6, out_specs=[a...  125 us
    pallas_call x1, Pallas kernels, mlp(): pl.pallas_call(mlp_kernel, in_specs=[any_, any_, pl.BlockSpec(memory_spac...  106 us

profile of v4, /device:TPU:0, one launch (start us, length us, event | category | flops | bytes accessed | tf_op | source)
XLA Modules:
  0.0 240.9 jit_solution(11765798428044360297)
XLA Ops:
  0.0 0.7 convert_element_type.3
  0.7 0.7 stack.9
  1.4 0.7 stack.10
  2.1 0.6 pad_maximum_fusion.2.g_ref
  2.7 1.9 fusion
  4.6 1.3 pad_maximum_fusion
  5.9 124.9 %att.1 = (bf16[1024,1536]{1,0:T(8,128)(2,1)}, bf16[512,1536]{1,0:T(8,128)(2,1)}) custom-call(bf16[1024,1536]{1,0:T(8,128)(2,1)} %x_h.1, bf16[2,1536]{1,0:T(2,128)(2,1)} %pad_maximum_fusion.2.g_ref, f32[1024,128]{1,0:T(8,128)} %get-tuple-element.12.cs_h, f32[1024,128]{1,0:T(8,128)} %get-tuple-element.13.sn_h, bf16[1536,768]{1,0:T(8,128)(2,1)} %wq_h.1, ...), custom_call_target="tpu_custom_call" | custom-call | flops 70000001024 | bytes 20971520 | tf_op jit(solution)/shard_map/att/pallas_call | solution.py:373
  130.8 106.4 %mlp.1 = bf16[1024,1536]{1,0:T(8,128)(2,1)} custom-call(bf16[1024,1536]{1,0:T(8,128)(2,1)} %get-tuple-element.7.h_h, bf16[512,1536]{1,0:T(8,128)(2,1)} %get-tuple-element.8.hpb_h, bf16[2,1536]{1,0:T(2,128)(2,1)} %pad_maximum_fusion.2.g_ref, bf16[1536,4480]{1,0:T(8,128)(2,1)} %w1_h.1, bf16[1536,4480]{1,0:T(8,128)(2,1)} %w3_h.1, bf16[4480,1536]{1,0:T(8,128)(2,1)} %w2_h.1), custom_call_target="tpu_custom_call" | custom-call | flops 84557168640 | bytes 165150720 | tf_op jit(solution)/shard_map/mlp/pallas_call | solution.py:513
  237.2 3.8 %copy.13 = bf16[1024,1536]{1,0:T(8,128)(2,1)} copy(bf16[1024,1536]{1,0:T(8,128)(2,1)} %mlp.1) | data formatting | bytes 6291456
  (1 shorter events, 0.0 us)

commit v5 on v4

--- a/solution.py
+++ b/solution.py
@@ -2,6 +2,7 @@
 import math
 import jax
 import jax.numpy as jnp
+import numpy as np
 from jax import lax
 from jax.experimental import pallas as pl
 from jax.experimental.pallas import tpu as pltpu
@@ -30,7 +31,7 @@
     return (vf * inv * g.astype(jnp.float32)).astype(jnp.bfloat16)
 
 
-def att_kernel(x_h, g_ref, cs_h, sn_h, wq_h, wk_h, wv_h, wo_h,
+def att_kernel(x_h, g_ref, pos_ref, fr_ref, wq_h, wk_h, wv_h, wo_h,
                h_ref, hp_ref,
                xv, csv, snv, wqb, wkb, wvb, wob, qb, kvb, m_s, al_s, acc_s, s0, s1, p0, p1, ob, hs,
                ld, ks, kr, ws, wr, hsem):
@@ -50,7 +51,7 @@
     def rc(src, dst, ss, rs, dev):
         return pltpu.make_async_remote_copy(src_ref=src, dst_ref=dst, send_sem=ss, recv_sem=rs, device_id=dev, device_id_type=MESH)
 
-    loads = [(x_h, xv), (wq_h, wqb.at[0]), (wk_h, wkb.at[0]), (wv_h, wvb.at[0]), (cs_h, csv), (sn_h, snv)]
+    loads = [(x_h, xv), (wq_h, wqb.at[0]), (wk_h, wkb.at[0]), (wv_h, wvb.at[0])]
     loads = [pltpu.make_async_copy(a, b, ld.at[i]) for i, (a, b) in enumerate(loads)]
     wol = pltpu.make_async_copy(wo_h, wob.at[pl.ds(0, QW)], ld.at[6])
     for l in loads:
@@ -93,8 +94,20 @@
         gs, ms, gd, md, dev = KV[n]
         return rc(kvb.at[gs, ms], kvb.at[gd, md], ks.at[gd, md], kr.at[gd, md], dev)
 
-    for n in ('k', 'v', 'qa'):
+    for n in ('k', 'v', 'qa', 'qb'):
         wcopy(n, 0).start()
+
+    sign = jnp.where(lax.broadcasted_iota(jnp.int32, (128, DH), 1) < DH // 2, -1.0, 1.0)
+
+    def table(i, _):
+        r = pl.ds(pl.multiple_of(i * 128, 128), 128)
+        p = jnp.broadcast_to(pos_ref[pl.ds(i, 1), :].astype(jnp.float32), (128, 128)).T
+        ang = p * fr_ref[...]
+        csv[r, :] = jnp.cos(ang)
+        snv[r, :] = jnp.sin(ang) * sign
+        return 0
+
+    lax.fori_loop(0, x_h.shape[0] // 128, table, 0)
     for l in loads:
         l.wait()
     wol.start()
@@ -102,7 +115,7 @@
     def front(g, do_q, do_kv):
         def blk(i, _):
             r = pl.ds(pl.multiple_of(i * 256, 256), 256)
-            a = rms(xv[r, :], g_ref[0:1, :])
+            a = rms(xv[r, :], g_ref[...].reshape(1, D))
             ww = ([wqb[g]] if do_q else []) + ([wkb[g], wvb[g]] if do_kv else [])
             y = jnp.dot(a, jnp.concatenate(ww, axis=1) if len(ww) > 1 else ww[0], preferred_element_type=jnp.float32)
             cc = csv[r, :]
@@ -134,9 +147,11 @@
     ones = jnp.ones((PC, 128), jnp.bfloat16)
 
     two = lambda g, ms: [(g, m, t) for m in ms for t in (3, 4)]
-    late = (2, 1, 3, 4, 6, 5, 7)
-    seq = [(0, 0, 0), (0, 0, 1), (0, 0, 2)] + two(0, (2, 4, 6, 1, 3, 5, 7)) + [(1, 0, 0)] + [(1, m, 3) for m in late]
-    seq = seq + [(1, 0, 1), (1, 0, 2)] + [(1, m, 4) for m in late]
+    own = lambda g: [(g, 0, 0), (g, 0, 1), (g, 0, 2)]
+    seq = own(0) + two(0, (2, 4, 6)) + own(1) + [(1, 2, 3), (0, 1, 3), (0, 3, 3), (1, 1, 3), (1, 3, 3), (0, 5, 3), (0, 7, 3)]
+    seq = seq + [(1, m, 3) for m in (4, 6, 5, 7)]
+    NB = len(seq)
+    seq = seq + [(1, m, 4) for m in (2, 1, 3, 4, 6, 5, 7)] + [(0, m, 4) for m in (1, 3, 5, 7)]
     NU = len(seq)
     codes = [g * 64 + m * 8 + t for g, m, t in seq]
 
@@ -204,7 +219,7 @@
 
     kw = lambda n: kcopy(n).wait_recv()
 
-    def act(u):
+    def act(u, prv):
         def at(i):
             return pl.when(u == i)
 
@@ -222,7 +237,6 @@
             front(1, False, True)
             kcopy('s').start()
             kcopy('y').start()
-            wcopy('qb', 0).start()
             kcopy('Y').start()
 
         @at(4)
@@ -236,81 +250,78 @@
         @at(6)
         def _():
             kw('XS')
+            wrecv('qb', 0)
+            wcopy('qb', 2).start()
+            wcopy('qb', 1).start()
 
         @at(8)
         def _():
+            wrecv('qa', 2)
+            wcopy('qa', 3).start()
+            wrecv('qb', 2)
+            wcopy('qb', 3).start()
             kw('y')
             kcopy('ys').start()
             kcopy('z').start()
-
-        @at(10)
-        def _():
-            kw('ys')
-
-        @at(11)
-        def _():
-            wrecv('qb', 0)
-            wcopy('qb', 2).start()
-            wcopy('qb', 1).start()
-            kcopy('x').start()
-            wcopy('o', 0).start()
-
-        @at(12)
-        def _():
-            kw('z')
-            kcopy('zs').start()
-
-        @at(14)
-        def _():
-            kw('zs')
-            wrecv('qa', 2)
-            wcopy('qa', 3).start()
-
-        @at(15)
-        def _():
-            kw('Y')
-            kcopy('YS').start()
-            kcopy('Z').start()
-
-        @at(16)
-        def _():
-            wrecv('qb', 2)
-            wcopy('qb', 3).start()
-            kw('s')
             for n in ('qa', 'qb'):
                 wrecv(n, 1)
                 wrecv(n, 3)
             front(1, True, False)
 
-        @at(19)
+        @at(9)
+        def _():
+            kcopy('x').start()
+            wcopy('o', 0).start()
+
+        @at(11)
+        def _():
+            kw('s')
+
+        @at(12)
+        def _():
+            kw('Y')
+            kcopy('YS').start()
+            kcopy('Z').start()
+
+        @at(13)
+        def _():
+            kw('ys')
+
+        @at(14)
+        def _():
+            kw('z')
+            kcopy('zs').start()
+
+        @at(15)
         def _():
             kw('YS')
 
-        @at(20)
-        def _():
+        @at(17)
+        def _():
+            kw('zs')
             kw('x')
             kcopy('xs').start()
 
-        @at(21)
+        @at(19)
         def _():
             kw('xs')
 
-        @at(22)
+        @at(20)
         def _():
             kw('Z')
             kcopy('ZS').start()
 
-        @at(23)
-        def _():
-            kw('ZS')
-
-        @at(24)
+        @at(21)
         def _():
             wrecv('o', 0)
             wcopy('o', 1).start()
-
-        @at(26)
-        def _():
+            kw('ZS')
+
+        @at(NB)
+        def _():
+            pv(prv, GRP - 1)
+            p1[...] = jnp.zeros_like(p1)
+            al_s[1] = jnp.ones_like(al_s[1])
             wol.wait()
             wrecv('o', 1)
             finalize(0)
@@ -322,9 +333,9 @@
 
     def body(u, carry):
         cc, pc = carry
-        act(u)
         nc = code_of(jnp.minimum(u + 1, NU - 1))
         cur, prv, nxt = decode(cc), decode(pc), decode(nc)
+        act(u, prv)
 
         def run(masked):
             for h in range(GRP):
@@ -365,14 +376,14 @@
             wcopy(n, hop).wait_send()
 
 
-def att(x, g, cs, sn, wq, wk, wv, wo):
+def att(x, g, pos, fr, wq, wk, wv, wo):
     n = x.shape[0]
     any_ = pl.BlockSpec(memory_space=pl.ANY)
     vm = pl.BlockSpec(memory_space=pltpu.VMEM)
     bf, f32 = jnp.bfloat16, jnp.float32
     return pl.pallas_call(
         att_kernel,
-        in_specs=[any_, vm] + [any_] * 6,
+        in_specs=[any_, vm, vm, vm] + [any_] * 4,
         out_specs=[any_, any_],
         out_shape=[jax.ShapeDtypeStruct((n, D), bf), jax.ShapeDtypeStruct((PC, D), bf)],
         scratch_shapes=[
@@ -385,14 +396,14 @@
             pltpu.SemaphoreType.DMA((9,)), pltpu.SemaphoreType.DMA((2, 8)), pltpu.SemaphoreType.DMA((2, 8)),
             pltpu.SemaphoreType.DMA((5, 4)), pltpu.SemaphoreType.DMA((5, 4)), pltpu.SemaphoreType.DMA((2,))],
         compiler_params=pltpu.CompilerParams(collective_id=0, has_side_effects=True, vmem_limit_bytes=VM),
-        cost_estimate=cost(70e9, 20 * 2**20), name="att")(x, g, cs, sn, wq, wk, wv, wo)
+        cost_estimate=cost(70e9, 20 * 2**20), name="att")(x, g, pos, fr, wq, wk, wv, wo)
 
 
 FU = 896
 ND = 768
 
 
-def mlp_kernel(h_h, hpb_h, g_ref, w1_h, w3_h, w2_h, o_h, hall, wb, w2b, hid, b_s, zs, zr, zo, ld, us, ds, zsem, zrm):
+def mlp_kernel(h_h, hpb_h, g_ref, w1_h, w3_h, w2_h, ob_h, oa_h, hall, wb, w2b, hid, b_s, zs, zr, zo, ld, us, ds, os_, zsem, zrm):
     j = lax.axis_index('tp')
     YP = {"tp": 1 - j}
     F = w1_h.shape[1]
@@ -423,23 +434,24 @@
     pl.semaphore_wait(bar, 1)
     hsend = rc(h_h.at[pl.ds(PC, PC)], hall.at[3], zsem.at[2], zrm.at[2])
     hsend.start()
-    zc = [rc(zs.at[i], zr.at[i], zsem.at[i], zrm.at[i]) for i in range(2)]
-    oc = [pltpu.make_async_copy(hall.at[i], o_h.at[pl.ds(i * PC, PC)], ld.at[3 + i]) for i in range(2)]
-
-    def finish(i):
-        zc[i].wait_recv()
-
+    hp = PC // 2
+    zc = [rc(zs.at[0], zr.at[0], zsem.at[0], zrm.at[0])]
+    zc = zc + [rc(zs.at[1, pl.ds(i * hp, hp)], zr.at[1, pl.ds(i * hp, hp)], zsem.at[(1, 3)[i]], zrm.at[(1, 3)[i]]) for i in range(2)]
+    outs = (ob_h, oa_h)
+    oc = [pltpu.make_async_copy(hall.at[i, pl.ds(r, hp)], outs[i].at[pl.ds(r, hp)], os_.at[i, r // hp]) for i in range(2) for r in (0, hp)]
+
+    def finish(i, part):
         def blk(t, _):
-            r = pl.ds(pl.multiple_of(t * 128, 128), 128)
+            r = pl.ds(pl.multiple_of(part * hp + t * 128, 128), 128)
             y = hall[i, r, :].astype(jnp.float32) + (zo[i, r, :] + zr[i, r, :].astype(jnp.float32))
             hall[i, r, :] = y.astype(jnp.bfloat16)
             return 0
 
-        lax.fori_loop(0, PC // 128, blk, 0)
-        oc[i].start()
+        lax.fori_loop(0, hp // 128, blk, 0)
+        oc[2 * i + part].start()
 
     def up_phase(n, idx, hb, more, pre):
-        b_s[...] = rms(hall[idx], g_ref[1:2, :])
+        b_s[...] = rms(hall[idx], g_ref[...].reshape(1, D))
 
         def step(t, _):
             slot = (n * NU_ + t) % 2
@@ -492,17 +504,23 @@
     hsend.wait_recv()
     up_phase(2, 3, 0, True, NDN % 2)
     down_phase(1, 3, 0, True)
+    zc[1].start()
+    zc[2].start()
+    down_phase(2, 0, 1, False)
+    zc[0].wait_recv()
+    finish(0, 0)
+    finish(0, 1)
     hl[2].wait()
-    zc[1].start()
-    down_phase(2, 0, 1, False)
-    finish(0)
     up_phase(3, 1, 0, False, (3 * NDN) % 2)
     down_phase(3, 1, 0, False)
-    finish(1)
+    for i in range(2):
+        zc[1 + i].wait_recv()
+        finish(1, i)
+    for o in oc:
+        o.wait()
     hsend.wait_send()
-    for i in range(2):
-        zc[i].wait_send()
-        oc[i].wait()
+    for z in zc:
+        z.wait_send()
 
 
 def mlp(h, hpb, g, w1, w3, w2):
@@ -513,14 +531,14 @@
     return pl.pallas_call(
         mlp_kernel,
         in_specs=[any_, any_, pl.BlockSpec(memory_space=pltpu.VMEM), any_, any_, any_],
-        out_specs=any_,
-        out_shape=jax.ShapeDtypeStruct((n, D), bf),
+        out_specs=[any_] * 2,
+        out_shape=[jax.ShapeDtypeStruct((PC, D), bf)] * 2,
         scratch_shapes=[
             pltpu.VMEM((4, PC, D), bf), pltpu.VMEM((2, D, 2 * FU), bf), pltpu.VMEM((2, f, ND), bf),
             pltpu.VMEM((2, PC, f), bf), pltpu.VMEM((PC, D), bf), pltpu.VMEM((2, PC, D), bf), pltpu.VMEM((2, PC, D), bf),
             pltpu.VMEM((2, PC, D), f32),
-            pltpu.SemaphoreType.DMA((5,)), pltpu.SemaphoreType.DMA((2, 2)), pltpu.SemaphoreType.DMA((2,)),
-            pltpu.SemaphoreType.DMA((3,)), pltpu.SemaphoreType.DMA((3,))],
+            pltpu.SemaphoreType.DMA((3,)), pltpu.SemaphoreType.DMA((2, 2)), pltpu.SemaphoreType.DMA((2,)), pltpu.SemaphoreType.DMA((2, 2)),
+            pltpu.SemaphoreType.DMA((4,)), pltpu.SemaphoreType.DMA((4,))],
         compiler_params=pltpu.CompilerParams(collective_id=1, has_side_effects=True, vmem_limit_bytes=VM),
         cost_estimate=cost(12 * n * D * f, 24 * D * f), name="mlp")(h, hpb, g, w1, w3, w2)
 
@@ -531,14 +549,9 @@
     row = P('tp', None)
 
     def local(x, pos, g1, g2, wq, wk, wv, wo, w1, w3, w2):
-        freq = 1.0 / (THETA ** (jnp.arange(0, DH, 2, dtype=jnp.float32) / DH))
-        ang = pos.astype(jnp.float32)[:, None] * freq
-        cs = jnp.cos(ang)
-        sn = jnp.sin(ang)
-        cs = jnp.concatenate([cs, cs], 1)
-        sn = jnp.concatenate([-sn, sn], 1)
-        gs = jnp.stack([g1, g2])
-        h, hp = att(x, gs, cs, sn, wq, wk, wv, wo)
-        return mlp(h, hp, gs, w1, w3, w2)
+        fr = 1.0 / (np.float32(THETA) ** (np.arange(0, DH, 2, dtype=np.float32) / np.float32(DH)))
+        fr = jnp.asarray(np.concatenate([fr, fr]).astype(np.float32).reshape(1, DH))
+        h, hp = att(x, g1, pos.reshape(-1, 128), fr, wq, wk, wv, wo)
+        return jnp.concatenate(mlp(h, hp, g2, w1, w3, w2), 0)
 
     return jax.shard_map(local, mesh=mesh, in_specs=(tok, P(('dp', 'cp', 'tp')), P(None), P(None), col, col, col, row, col, col, row), out_specs=tok, check_vma=False)

time: 241 us -> 228 us (0.946)
  Pallas kernels: 231 us -> 224 us
  local copies, waits for them, and re-layouts: 5.14 us -> 0 us
    pallas_call x1, Pallas kernels: 125 us -> 119 us  [att(): pl.pallas_call(att_kernel, in_specs=[any_, vm, vm, vm] + [any_] * 4, out_...]
    unnamed x1 -> x0, local copies, waits for them, and re-layouts: 3.76 us -> none
    concatenate x1, other arithmetic: 1.31 us -> 3.75 us  [local(): return jnp.concatenate(mlp(h, hp, g2, w1, w3, w2), 0)]
where the time goes in v5:
time: 228 us
  Pallas kernels  224 us (98%)
  other arithmetic  3.75 us (2%)
    pallas_call x1, Pallas kernels, att(): pl.pallas_call(att_kernel, in_specs=[any_, vm, vm, vm] + [any_] * 4, out_...  119 us
    pallas_call x1, Pallas kernels, mlp(): pl.pallas_call(mlp_kernel, in_specs=[any_, any_, pl.BlockSpec(memory_spac...  105 us

profile of v5, /device:TPU:0, one launch (start us, length us, event | category | flops | bytes accessed | tf_op | source)
XLA Modules:
  0.0 228.1 jit_solution(9382840316288226180)
XLA Ops:
  0.0 119.4 %att.1 = (bf16[1024,1536]{1,0:T(8,128)(2,1)}, bf16[512,1536]{1,0:T(8,128)(2,1)}) custom-call(bf16[1024,1536]{1,0:T(8,128)(2,1)} %x_h.1, bf16[1536]{0:T(1024)(128)(2,1)} %g_ref.2, s32[8,128]{1,0:T(8,128)} %bitcast.1, f32[1,128]{1,0:T(1,128)} %constant.2.clone.fr_ref, bf16[1536,768]{1,0:T(8,128)(2,1)} %wq_h.1, bf16[1536,128]{1,0:T(8,128)(2,1)} %wk_h.1, ...), custom_call_target="tpu_custom_call" | custom-call | flops 70000001024 | bytes 20971520 | tf_op jit(solution)/shard_map/att/pallas_call | solution.py:384
  119.4 104.9 %mlp.1 = (bf16[512,1536]{1,0:T(8,128)(2,1)}, bf16[512,1536]{1,0:T(8,128)(2,1)}) custom-call(bf16[1024,1536]{1,0:T(8,128)(2,1)} %get-tuple-element.9.h_h, bf16[512,1536]{1,0:T(8,128)(2,1)} %get-tuple-element.10.hpb_h, bf16[1536]{0:T(1024)(128)(2,1)} %g_ref.3, bf16[1536,4480]{1,0:T(8,128)(2,1)} %w1_h.1, bf16[1536,4480]{1,0:T(8,128)(2,1)} %w3_h.1, ...), custom_call_target="tpu_custom_call" | custom-call | flops 84557168640 | bytes 165150720 | tf_op jit(solution)/shard_map/mlp/pallas_call | solution.py:531
  224.3 3.7 %pad_maximum_fusion = bf16[1024,1536]{1,0:T(8,128)(2,1)} fusion(bf16[512,1536]{1,0:T(8,128)(2,1)} %get-tuple-element.12, bf16[512,1536]{1,0:T(8,128)(2,1)} %get-tuple-element.11), kind=kLoop, calls=%fused_computation | loop fusion | flops 6291456 | bytes 6291456 | tf_op jit(solution)/shard_map/concatenate | solution.py:555

commit v6 on v5

--- a/solution.py
+++ b/solution.py
@@ -1,5 +1,6 @@
 import functools
 import math
+import re
 import jax
 import jax.numpy as jnp
 import numpy as np
@@ -85,13 +86,12 @@
         i = WI[n]
         rc(dst.at[rg], dst.at[rg], ws.at[i, hop], wr.at[i, hop], (YP, SIB, XP, SIB)[hop]).wait_recv()
 
-    KV = {'S': (0, 0, 0, 2, SIB), 'X': (0, 0, 0, 4, XP), 'Y': (0, 0, 1, 1, YP), 'XS': (0, 4, 0, 6, SIB),
-          'YS': (1, 1, 1, 3, SIB), 'Z': (1, 1, 1, 5, XP), 'ZS': (1, 5, 1, 7, SIB),
-          's': (1, 0, 1, 2, SIB), 'x': (1, 0, 1, 4, XP), 'y': (1, 0, 0, 1, YP), 'xs': (1, 4, 1, 6, SIB),
-          'ys': (0, 1, 0, 3, SIB), 'z': (0, 1, 0, 5, XP), 'zs': (0, 5, 0, 7, SIB)}
+    KV = {'S': '0002S', 'X': '0004X', 'Y': '0011Y', 'XS': '0406S', 'YS': '1113S', 'Z': '1115X', 'ZS': '1517S',
+          's': '1012S', 'x': '1014X', 'y': '1001Y', 'xs': '1416S', 'ys': '0103S', 'z': '0105X', 'zs': '0507S'}
+    PEER = {'S': SIB, 'X': XP, 'Y': YP}
 
     def kcopy(n):
-        gs, ms, gd, md, dev = KV[n]
+        (gs, ms, gd, md), dev = map(int, KV[n][:-1]), PEER[KV[n][-1]]
         return rc(kvb.at[gs, ms], kvb.at[gd, md], ks.at[gd, md], kr.at[gd, md], dev)
 
     for n in ('k', 'v', 'qa', 'qb'):
@@ -146,14 +146,11 @@
     p1[...] = jnp.zeros_like(p1)
     ones = jnp.ones((PC, 128), jnp.bfloat16)
 
-    two = lambda g, ms: [(g, m, t) for m in ms for t in (3, 4)]
-    own = lambda g: [(g, 0, 0), (g, 0, 1), (g, 0, 2)]
-    seq = own(0) + two(0, (2, 4, 6)) + own(1) + [(1, 2, 3), (0, 1, 3), (0, 3, 3), (1, 1, 3), (1, 3, 3), (0, 5, 3), (0, 7, 3)]
-    seq = seq + [(1, m, 3) for m in (4, 6, 5, 7)]
-    NB = len(seq)
-    seq = seq + [(1, m, 4) for m in (2, 1, 3, 4, 6, 5, 7)] + [(0, m, 4) for m in (1, 3, 5, 7)]
-    NU = len(seq)
-    codes = [g * 64 + m * 8 + t for g, m, t in seq]
+    EARLY = '000001002023024043044063064100123013033113133053073143163101' + '102153173'
+    LATE = '124114134144164154174014034054074'
+    NB = len(EARLY) // 3
+    codes = [int(c[0]) * 64 + int(c[1]) * 8 + int(c[2]) for c in re.findall('...', EARLY + LATE)]
+    NU = len(codes)
 
     def code_of(u):
         v = jnp.int32(codes[0])
@@ -210,11 +207,16 @@
             rx = pl.ds(pl.multiple_of(qp * PC + i * 256, 256), 256)
             y = jnp.dot(ob[r, :], wob[...], preferred_element_type=jnp.float32)
             hs[rx, :] = (xv[rx, :].astype(jnp.float32) + y).astype(jnp.bfloat16)
+            if qp == 0:
+                hcopy(i).start()
             return 0
 
         lax.fori_loop(0, 2, blk, 0)
 
-    hcopy = rc(hs.at[pl.ds(0, PC)], hp_ref, hsem.at[0], hsem.at[1], YP)
+    def hcopy(i):
+        r = pl.ds(pl.multiple_of(i * 256, 256), 256)
+        return rc(hs.at[r], hp_ref.at[r], hsem.at[0, i], hsem.at[1, i], YP)
+
     hout = [pltpu.make_async_copy(hs.at[pl.ds(i * PC, PC)], h_ref.at[pl.ds(i * PC, PC)], ld.at[7 + i]) for i in range(2)]
 
     kw = lambda n: kcopy(n).wait_recv()
@@ -272,37 +274,37 @@
         def _():
             kcopy('x').start()
             wcopy('o', 0).start()
-
-        @at(11)
-        def _():
             kw('s')
 
-        @at(12)
+        @at(10)
         def _():
             kw('Y')
             kcopy('YS').start()
             kcopy('Z').start()
 
-        @at(13)
+        @at(11)
         def _():
             kw('ys')
 
-        @at(14)
+        @at(12)
         def _():
             kw('z')
             kcopy('zs').start()
 
+        @at(13)
+        def _():
+            kw('YS')
+
         @at(15)
         def _():
-            kw('YS')
-
-        @at(17)
-        def _():
             kw('zs')
+
+        @at(16)
+        def _():
             kw('x')
             kcopy('xs').start()
 
-        @at(19)
+        @at(17)
         def _():
             kw('xs')
 
@@ -325,7 +327,6 @@
             wol.wait()
             wrecv('o', 1)
             finalize(0)
-            hcopy.start()
             hout[0].start()
 
     e0 = decode(jnp.int32(codes[0]))
@@ -365,8 +366,9 @@
     pv(decode(fin[1]), GRP - 1)
     finalize(1)
     hout[1].start()
-    hcopy.wait_recv()
-    hcopy.wait_send()
+    for i in range(2):
+        hcopy(i).wait_recv()
+        hcopy(i).wait_send()
     for o in hout:
         o.wait()
     for n in KV:
@@ -394,7 +396,7 @@
             pltpu.VMEM((PC, PC), f32), pltpu.VMEM((PC, PC), f32), pltpu.VMEM((PC, PC), bf), pltpu.VMEM((PC, PC), bf),
             pltpu.VMEM((PC, D), bf), pltpu.VMEM((n, D), bf),
             pltpu.SemaphoreType.DMA((9,)), pltpu.SemaphoreType.DMA((2, 8)), pltpu.SemaphoreType.DMA((2, 8)),
-            pltpu.SemaphoreType.DMA((5, 4)), pltpu.SemaphoreType.DMA((5, 4)), pltpu.SemaphoreType.DMA((2,))],
+            pltpu.SemaphoreType.DMA((5, 4)), pltpu.SemaphoreType.DMA((5, 4)), pltpu.SemaphoreType.DMA((2, 2))],
         compiler_params=pltpu.CompilerParams(collective_id=0, has_side_effects=True, vmem_limit_bytes=VM),
         cost_estimate=cost(70e9, 20 * 2**20), name="att")(x, g, pos, fr, wq, wk, wv, wo)
 

time: 228 us -> 227 us (level)
  no operation moved by 1% of the time
where the time goes in v6:
time: 227 us
  Pallas kernels  223 us (98%)
  other arithmetic  3.75 us (2%)
    pallas_call x1, Pallas kernels, att(): pl.pallas_call(att_kernel, in_specs=[any_, vm, vm, vm] + [any_] * 4, out_...  118 us
    pallas_call x1, Pallas kernels, mlp(): pl.pallas_call(mlp_kernel, in_specs=[any_, any_, pl.BlockSpec(memory_spac...  105 us

profile of v6, /device:TPU:0, one launch (start us, length us, event | category | flops | bytes accessed | tf_op | source)
XLA Modules:
  0.0 226.7 jit_solution(7306381782258223072)
XLA Ops:
  0.0 118.0 %att.1 = (bf16[1024,1536]{1,0:T(8,128)(2,1)}, bf16[512,1536]{1,0:T(8,128)(2,1)}) custom-call(bf16[1024,1536]{1,0:T(8,128)(2,1)} %x_h.1, bf16[1536]{0:T(1024)(128)(2,1)} %g_ref.2, s32[8,128]{1,0:T(8,128)} %bitcast.1, f32[1,128]{1,0:T(1,128)} %constant.2.clone.fr_ref, bf16[1536,768]{1,0:T(8,128)(2,1)} %wq_h.1, bf16[1536,128]{1,0:T(8,128)(2,1)} %wk_h.1, ...), custom_call_target="tpu_custom_call" | custom-call | flops 70000001024 | bytes 20971520 | tf_op jit(solution)/shard_map/att/pallas_call | solution.py:386
  118.0 104.9 %mlp.1 = (bf16[512,1536]{1,0:T(8,128)(2,1)}, bf16[512,1536]{1,0:T(8,128)(2,1)}) custom-call(bf16[1024,1536]{1,0:T(8,128)(2,1)} %get-tuple-element.9.h_h, bf16[512,1536]{1,0:T(8,128)(2,1)} %get-tuple-element.10.hpb_h, bf16[1536]{0:T(1024)(128)(2,1)} %g_ref.3, bf16[1536,4480]{1,0:T(8,128)(2,1)} %w1_h.1, bf16[1536,4480]{1,0:T(8,128)(2,1)} %w3_h.1, ...), custom_call_target="tpu_custom_call" | custom-call | flops 84557168640 | bytes 165150720 | tf_op jit(solution)/shard_map/mlp/pallas_call | solution.py:533
  222.9 3.7 %pad_maximum_fusion = bf16[1024,1536]{1,0:T(8,128)(2,1)} fusion(bf16[512,1536]{1,0:T(8,128)(2,1)} %get-tuple-element.12, bf16[512,1536]{1,0:T(8,128)(2,1)} %get-tuple-element.11), kind=kLoop, calls=%fused_computation | loop fusion | flops 6291456 | bytes 6291456 | tf_op jit(solution)/shard_map/concatenate | solution.py:557

commit v7 on v6

--- a/solution.py
+++ b/solution.py
@@ -197,14 +197,13 @@
         acc_s[g, qp, h] = acc_s[g, qp, h] * jnp.tile(al_s[h % 2], (1, 2)) + y
 
     def finalize(qp):
-        for g in range(2):
-            for h in range(GRP):
-                a = acc_s[g, qp, h]
-                ob[:, (g * GRP + h) * DH:(g * GRP + h + 1) * DH] = (a[:, :128] / a[:, 128:]).astype(jnp.bfloat16)
-
         def blk(i, _):
             r = pl.ds(pl.multiple_of(i * 256, 256), 256)
             rx = pl.ds(pl.multiple_of(qp * PC + i * 256, 256), 256)
+            for g in range(2):
+                for h in range(GRP):
+                    a = acc_s[g, qp, h, r, :]
+                    ob[r, (g * GRP + h) * DH:(g * GRP + h + 1) * DH] = (a[:, :128] / a[:, 128:]).astype(jnp.bfloat16)
             y = jnp.dot(ob[r, :], wob[...], preferred_element_type=jnp.float32)
             hs[rx, :] = (xv[rx, :].astype(jnp.float32) + y).astype(jnp.bfloat16)
             if qp == 0:

time: 227 us -> 226 us (level)
  no operation moved by 1% of the time
where the time goes in v7:
time: 226 us
  Pallas kernels  223 us (99%)
  other arithmetic  3.75 us (2%)
    pallas_call x1, Pallas kernels, att(): pl.pallas_call(att_kernel, in_specs=[any_, vm, vm, vm] + [any_] * 4, out_...  118 us
    pallas_call x1, Pallas kernels, mlp(): pl.pallas_call(mlp_kernel, in_specs=[any_, any_, pl.BlockSpec(memory_spac...  105 us

profile of v7, /device:TPU:0, one launch (start us, length us, event | category | flops | bytes accessed | tf_op | source)
XLA Modules:
  0.0 226.3 jit_solution(15217100279193145892)
XLA Ops:
  0.0 117.6 %att.1 = (bf16[1024,1536]{1,0:T(8,128)(2,1)}, bf16[512,1536]{1,0:T(8,128)(2,1)}) custom-call(bf16[1024,1536]{1,0:T(8,128)(2,1)} %x_h.1, bf16[1536]{0:T(1024)(128)(2,1)} %g_ref.2, s32[8,128]{1,0:T(8,128)} %bitcast.1, f32[1,128]{1,0:T(1,128)} %constant.2.clone.fr_ref, bf16[1536,768]{1,0:T(8,128)(2,1)} %wq_h.1, bf16[1536,128]{1,0:T(8,128)(2,1)} %wk_h.1, ...), custom_call_target="tpu_custom_call" | custom-call | flops 70000001024 | bytes 20971520 | tf_op jit(solution)/shard_map/att/pallas_call | solution.py:385
  117.6 104.9 %mlp.1 = (bf16[512,1536]{1,0:T(8,128)(2,1)}, bf16[512,1536]{1,0:T(8,128)(2,1)}) custom-call(bf16[1024,1536]{1,0:T(8,128)(2,1)} %get-tuple-element.9.h_h, bf16[512,1536]{1,0:T(8,128)(2,1)} %get-tuple-element.10.hpb_h, bf16[1536]{0:T(1024)(128)(2,1)} %g_ref.3, bf16[1536,4480]{1,0:T(8,128)(2,1)} %w1_h.1, bf16[1536,4480]{1,0:T(8,128)(2,1)} %w3_h.1, ...), custom_call_target="tpu_custom_call" | custom-call | flops 84557168640 | bytes 165150720 | tf_op jit(solution)/shard_map/mlp/pallas_call | solution.py:532
  222.5 3.7 %pad_maximum_fusion = bf16[1024,1536]{1,0:T(8,128)(2,1)} fusion(bf16[512,1536]{1,0:T(8,128)(2,1)} %get-tuple-element.12, bf16[512,1536]{1,0:T(8,128)(2,1)} %get-tuple-element.11), kind=kLoop, calls=%fused_computation | loop fusion | flops 6291456 | bytes 6291456 | tf_op jit(solution)/shard_map/concatenate | solution.py:556
